TPU v7x, 512 devices: a whole 4x8x8 slice. The times are simulated.
512 devices in a mesh: slab: 128 (over y, x, z_hi, core), col: 4 (over z_lo).
Axes of the slice: x: 4, y: 8, z: 8 (z_hi: 2, z_lo: 4; z = z_hi * 4 + z_lo), core: 2. Of those that a mesh axis runs over, the one named last changes fastest.
Arguments:
- volume: bfloat16 [128, 512, 6144], P('slab', 'col'), may hold values from -6 to 6
- detector_row_weight: bfloat16 [128, 512], P(None, 'col'), may hold values from -0.25 to 0.25
- tile_bank: bfloat16 [4, 128, 128], replicated, may hold values from -0.5 to 0.5
- tile_class: int32 [128], replicated, may hold values from 0 to 3
- tile_shift: int32 [128], replicated, may hold values from 0 to 47
- owner_angle: int32 [128], replicated, may hold values from 0 to 127, each once
- measured: bfloat16 [128, 128, 6144], P('slab', None, 'col'), may hold values from -6 to 6
- window_slice: int32 [128], P('slab'), may hold values from -4 to 0
- window_col: int32 [128], P('slab'), may hold values from -32 to 16
Outputs:
- projection: bfloat16 [128, 128, 6144], P('slab', None, 'col')
- correlation: float32 [128, 4, 16], P('slab')
- shifts: float32 [2, 128], P(None, 'slab')
Inputs may be any that keep to these rules, and one draw needn't show every extreme that they name: `owner_angle`: every angle stands in exactly one slot.
All inputs are finite; a program needn't handle non-finite values.
Results may differ from a plain program's by a relative error of at most 0.0095.
Values may be sent and summed in bfloat16 or wider, within the bound.
No kernel may reach another device: no remote copies, remote signals or barrier semaphores. Data moves between devices by JAX's collectives and lax.ppermute only.
A program may use at most 64 MiB of HBM per device.

v0:
```python
import math

import jax
import jax.numpy as jnp
from jax import lax
from jax.sharding import PartitionSpec as P

LAG = 32
WU = 16
LAGZ = 4
WZ = 4


def split_up(value, dim, peers):
    lengths = value.shape
    parts = value.reshape(*lengths[:dim], peers, lengths[dim] // peers, *lengths[dim + 1 :])
    return jnp.moveaxis(parts, dim, 0)


def summed_on_arrival(value, axis, dim):
    peers = lax.axis_size(axis)
    parts = lax.all_to_all(split_up(value, dim, peers), axis, 0, 0, tiled=True)
    return jnp.sum(parts.astype(jnp.float32), axis=0)


def padded_2(block, sides, width):
    for axis, dim in sides:
        count = lax.axis_size(axis)
        forward = [(i, i + 1) for i in range(count - 1)]
        forward.append((count - 1, 0))
        backward = [(target, source) for source, target in forward]
        low = lax.ppermute(
            lax.slice_in_dim(block, block.shape[dim] - width, None, axis=dim), axis, forward
        )
        high = lax.ppermute(lax.slice_in_dim(block, 0, width, axis=dim), axis, backward)
        block = jnp.concatenate([low, block, high], axis=dim)
    return block


def correlate_one(owned_slot, padded_slot, start_slice, start_col, diagonal_mask, norm_factor):
    slice_count = owned_slot.shape[0]
    columns = owned_slot.shape[1]
    doubled = jnp.concatenate([padded_slot, padded_slot], axis=0)
    aligned = lax.dynamic_slice_in_dim(doubled, start_slice % slice_count, slice_count, 0)
    offsets = LAG + start_col + jnp.arange(WU, dtype=jnp.int32)

    def one_lag(position):
        piece = lax.dynamic_slice_in_dim(aligned, position, columns, 1)
        return lax.dot_general(
            owned_slot, piece, (((1,), (1,)), ((), ())), preferred_element_type=jnp.float32
        )

    gramians = lax.map(one_lag, offsets)
    return (
        jnp.einsum("bzy,azy->ab", gramians, diagonal_mask, precision=lax.Precision.HIGHEST)
        * norm_factor
    )


def local(
    volume,
    detector_row_weight,
    tile_bank,
    tile_class,
    tile_shift,
    owner_angle,
    measured,
    window_slice,
    window_col,
):
    slices, beam_rows, columns = volume.shape
    angles = detector_row_weight.shape[0]
    tile_size = tile_bank.shape[1]
    tile_count = columns // tile_size
    block_size = math.gcd(angles, 32)
    block_count = angles // block_size
    chosen = jnp.take(detector_row_weight, owner_angle, axis=0).reshape(
        block_count, block_size, beam_rows
    )
    openings = (tile_count - jnp.take(tile_shift, owner_angle)).reshape(block_count, block_size)
    classes = jnp.take(tile_class, owner_angle).reshape(block_count, block_size)

    def project_block(item):
        weights_block, openings_block, classes_block = item
        ray_sums = jnp.einsum(
            "ky,syx->ksx", weights_block, volume, preferred_element_type=jnp.float32
        ).astype(jnp.bfloat16)
        tiled = ray_sums.reshape(block_size, slices, tile_count, tile_size)
        doubled = jnp.concatenate([tiled, tiled], axis=2)
        rolled = jax.vmap(
            lambda planes, opening: lax.dynamic_slice_in_dim(planes, opening, tile_count, 1)
        )(doubled, openings_block)
        system_operators = jnp.take(tile_bank, classes_block, axis=0)
        return jnp.einsum(
            "kstc,kcd->kstd", rolled, system_operators, preferred_element_type=jnp.float32
        ).reshape(block_size, slices, columns)

    spread = lax.map(project_block, (chosen, openings, classes)).reshape(angles, slices, columns)
    summed = summed_on_arrival(spread.astype(jnp.bfloat16), "col", 2).astype(jnp.bfloat16)
    owned = lax.all_to_all(summed, "slab", split_axis=0, concat_axis=1, tiled=True)
    padded = padded_2(measured, (("col", 2),), LAG)
    slot_count, slice_grand_sum, quarter = owned.shape
    norm_factor = 1.0 / math.sqrt(slice_grand_sum * quarter * lax.axis_size("col"))
    slice_range = jnp.arange(slice_grand_sum, dtype=jnp.int32)
    lag_slices = jnp.arange(WZ, dtype=jnp.int32)
    lag_columns = jnp.arange(WU, dtype=jnp.int32)
    diagonal_mask = (
        slice_range[None, None, :]
        == (slice_range[None, :, None] + lag_slices[:, None, None]) % slice_grand_sum
    ).astype(jnp.float32)
    search_regions = jnp.stack(
        [
            correlate_one(
                owned[0], padded[0], window_slice[0], window_col[0], diagonal_mask, norm_factor
            )
        ]
    )
    totals = lax.psum(search_regions, "col")
    weight_grid = totals * totals
    along_slices = (window_slice[:, None] + lag_slices[None, :]).astype(jnp.float32) / LAGZ
    along_columns = (window_col[:, None] + lag_columns[None, :]).astype(jnp.float32) / LAG
    denominator = jnp.mean(weight_grid, axis=(1, 2)) + 1e-06
    shift_slices = jnp.mean(weight_grid * along_slices[:, :, None], axis=(1, 2)) / denominator
    shift_columns = jnp.mean(weight_grid * along_columns[:, None, :], axis=(1, 2)) / denominator
    return (owned, totals, jnp.stack([shift_slices, shift_columns]))


def solution(mesh):
    return jax.shard_map(
        local,
        mesh=mesh,
        in_specs=(
            P("slab", "col", None),
            P(None, "col"),
            P(),
            P(),
            P(),
            P(),
            P("slab", None, "col"),
            P("slab"),
            P("slab"),
        ),
        out_specs=(P("slab", None, "col"), P("slab", None, None), P(None, "slab")),
        check_vma=False,
    )
```

profile of v0, /device:TPU:2, one launch (start us, length us, event | category | flops | bytes accessed | tf_op | source)
XLA Modules:
  0.0 215.1 jit_solution(11668494151956539573)
XLA Ops:
  1.3 1.6 gather_fusion.4
  4.4 1.6 gather_fusion.3
  6.2 37.0 %while.20 = (s32[]{:T(128)}, bf16[4,32,1,6144]{3,1,2,0:T(8,128)(2,1)}, bf16[4,32,128]{2,1,0:T(8,128)(2,1)S(1)}, bf16[1,128,6144]{2,1,0:T(8,128)(2,1)}, s32[4,32]...) while((s32[]{:T(128)}, bf16[4,32,1,6144]{3,1,2,0:T(8,128)(2,1)}, ...), condition=%wide.region_1.3_spmd, body=%wide.region_0.0_spmd.sunk | while | flops 101778976 | bytes 11548733 | solution.py:98
  6.3 1.7 fusion.41
  8.9 2.0 pad_maximum_fusion.3
  11.0 2.2 %gather_fusion.1 = bf16[32,48,128]{2,0,1:T(8,128)(2,1)S(1)} fusion(bf16[32,1,96,128]{3,1,0,2:T(2,128)(2,1)S(1)} %pad_maximum_fusion.3, s32[32]{0:T(128)S(1)} %get-tuple-element.177), kind=kCustom, calls=%fused_computation.2.clone.1 | custom fusion | bytes 786944 | tf_op jit(solution)/shard_map/while/body/eval_jaxpr/vmap()/gather | solution.py:91
  15.5 1.7 fusion.41
  18.2 2.0 pad_maximum_fusion.3
  20.2 2.2 %gather_fusion.1 = bf16[32,48,128]{2,0,1:T(8,128)(2,1)S(1)} fusion(bf16[32,1,96,128]{3,1,0,2:T(2,128)(2,1)S(1)} %pad_maximum_fusion.3, s32[32]{0:T(128)S(1)} %get-tuple-element.177), kind=kCustom, calls=%fused_computation.2.clone.1 | custom fusion | bytes 786944 | tf_op jit(solution)/shard_map/while/body/eval_jaxpr/vmap()/gather | solution.py:91
  24.7 1.7 fusion.41
  27.4 2.0 pad_maximum_fusion.3
  29.5 2.2 %gather_fusion.1 = bf16[32,48,128]{2,0,1:T(8,128)(2,1)S(1)} fusion(bf16[32,1,96,128]{3,1,0,2:T(2,128)(2,1)S(1)} %pad_maximum_fusion.3, s32[32]{0:T(128)S(1)} %get-tuple-element.177), kind=kCustom, calls=%fused_computation.2.clone.1 | custom fusion | bytes 786944 | tf_op jit(solution)/shard_map/while/body/eval_jaxpr/vmap()/gather | solution.py:91
  34.0 1.7 fusion.41
  36.7 2.0 pad_maximum_fusion.3
  38.7 2.2 %gather_fusion.1 = bf16[32,48,128]{2,0,1:T(8,128)(2,1)S(1)} fusion(bf16[32,1,96,128]{3,1,0,2:T(2,128)(2,1)S(1)} %pad_maximum_fusion.3, s32[32]{0:T(128)S(1)} %get-tuple-element.177), kind=kCustom, calls=%fused_computation.2.clone.1 | custom fusion | bytes 786944 | tf_op jit(solution)/shard_map/while/body/eval_jaxpr/vmap()/gather | solution.py:91
  43.2 3.6 %convert_element_type.41 = bf16[128,1,4,1536]{3,2,0,1:T(4,128)(2,1)S(1)} reshape(bf16[4,32,1,6144]{3,1,2,0:T(8,128)(2,1)} %get-tuple-element.68) | data formatting | bytes 3145728 | tf_op jit(solution)/shard_map/convert_element_type | solution.py:99
  47.1 44.0 %all_to_all.17 = bf16[4,128,1,1536]{3,1,2,0:T(8,128)(2,1)S(1)} all-to-all(bf16[4,128,1,1536]{3,1,2,0:T(8,128)(2,1)S(1)} %copy.27), channel_id=1, replica_groups=mesh['slab'=128,'col'=4] {'col'}, dimensions={0} | all-to-all | bytes 3145728 | tf_op jit(solution)/shard_map/all_to_all | solution.py:22
  93.6 17.2 %all-to-all-start.1 = ((bf16[128,2,768]{2,1,0:T(2,128)(2,1)}), bf16[128,2,768]{2,1,0:T(2,128)(2,1)S(1)}, u32[]{:S(2)}, u32[]{:S(2)}) async-start(bf16[128,2,768]{2,1,0:T(2,128)(2,1)} %reshape.255), calls=%async_computation.1 | async-start | bytes 786432 | tf_op jit(solution)/shard_map/all_to_all | solution.py:100
  110.9 2.1 collective-permute-start
  113.0 5.7 %collective-permute-start.1 = (bf16[1,128,32]{2,1,0:T(8,128)(2,1)S(1)}, bf16[1,128,32]{2,1,0:T(8,128)(2,1)S(1)}, u32[]{:S(2)}, u32[]{:S(2)}) collective-permute-start(bf16[1,128,32]{2,1,0:T(8,128)(2,1)S(1)} %get-tuple-element.103), channel_id=1, source_target_pairs={{1,0},{2,1},{3,2},{0,3},{5,4},{6,5},{7,6},{4,7},{9,8},{10,9},{11,1... | collective-permute-start | bytes 24584 | tf_op jit(solution)/shard_map/ppermute | solution.py:35
  120.4 2.3 %collective-permute-done.1 = bf16[1,128,32]{2,1,0:T(8,128)(2,1)S(1)} collective-permute-done((bf16[1,128,32]{2,1,0:T(8,128)(2,1)S(1)}, bf16[1,128,32]{2,1,0:T(8,128)(2,1)S(1)}, u32[]{:S(2)}, u32[]{:S(2)}) %collective-permute-start.1) | collective-permute-done | bytes 8224 | tf_op jit(solution)/shard_map/ppermute | solution.py:35
  123.5 7.9 %all-to-all-done.1 = bf16[128,2,768]{2,1,0:T(2,128)(2,1)S(1)} async-done(((bf16[128,2,768]{2,1,0:T(2,128)(2,1)}), bf16[128,2,768]{2,1,0:T(2,128)(2,1)S(1)}, u32[]{:S(2)}, u32[]{:S(2)}) %all-to-all-start.1) | async-done | bytes 393248 | tf_op jit(solution)/shard_map/all_to_all | solution.py:100
  131.8 69.3 %while.21 = (s32[]{:T(128)}, f32[16,128,128]{1,0,2:T(8,128)S(1)}, s32[16]{0:T(128)S(1)}, bf16[128,1600]{1,0:T(8,128)(2,1)S(1)}, bf16[128,1536]{1,0:T(8,128)(2,1)S(1)}, /*index=5*/s32[]{:T(128)}, s32[]{:T(128)}, s32[]{:T(128)}) while((s32[]{:T(128)}, f32[16,128,128]{1,0,2:T(8,128)S(1)}, s32[16]{0:T(128)S(1)}, bf16[128,1600]{1,0:T(8,128)(2,1)S(1)}, ...), condition=%wide.region_4.6_spmd, body=%wide.region_3.5_spmd.sunk | while | flops 50331652 | bytes 983179 | solution.py:53
  201.9 9.9 %psum.7 = f32[1,4,16]{2,1,0:T(4,128)S(1)} all-reduce(f32[1,4,16]{2,1,0:T(4,128)S(1)} %fusion.19), channel_id=1, replica_groups=mesh['slab'=128,'col'=4] {'col'}, use_global_device_ids=true, to_apply=%region_5.7 | all-reduce | flops 64 | bytes 512 | tf_op jit(solution)/shard_map/psum | solution.py:118
  (129 shorter events, 59.2 us)
Async XLA Ops:
  0.6 3.0 %copy-start = (bf16[128,128]{1,0:T(8,128)(2,1)S(1)}, bf16[128,128]{1,0:T(8,128)(2,1)}, u32[]{:S(2)}) copy-start(bf16[128,128]{1,0:T(8,128)(2,1)} %param.16) | copy-start | bytes 98308
  11.0 2.3 %copy-start.1 = (bf16[4,128,128]{2,1,0:T(8,128)(2,1)S(1)}, bf16[4,128,128]{2,1,0:T(8,128)(2,1)}, u32[]{:S(2)}) copy-start(bf16[4,128,128]{2,1,0:T(8,128)(2,1)} %get-tuple-element.205) | copy-start | bytes 393220 | tf_op jit(solution)/shard_map/while
  20.2 2.3 %copy-start.1 = (bf16[4,128,128]{2,1,0:T(8,128)(2,1)S(1)}, bf16[4,128,128]{2,1,0:T(8,128)(2,1)}, u32[]{:S(2)}) copy-start(bf16[4,128,128]{2,1,0:T(8,128)(2,1)} %get-tuple-element.205) | copy-start | bytes 393220 | tf_op jit(solution)/shard_map/while
  29.5 2.3 %copy-start.1 = (bf16[4,128,128]{2,1,0:T(8,128)(2,1)S(1)}, bf16[4,128,128]{2,1,0:T(8,128)(2,1)}, u32[]{:S(2)}) copy-start(bf16[4,128,128]{2,1,0:T(8,128)(2,1)} %get-tuple-element.205) | copy-start | bytes 393220 | tf_op jit(solution)/shard_map/while
  38.7 2.3 %copy-start.1 = (bf16[4,128,128]{2,1,0:T(8,128)(2,1)S(1)}, bf16[4,128,128]{2,1,0:T(8,128)(2,1)}, u32[]{:S(2)}) copy-start(bf16[4,128,128]{2,1,0:T(8,128)(2,1)} %get-tuple-element.205) | copy-start | bytes 393220 | tf_op jit(solution)/shard_map/while
  91.4 19.5 %copy-start.3 = (bf16[1,128,1536]{2,1,0:T(8,128)(2,1)S(1)}, bf16[1,128,1536]{2,1,0:T(8,128)(2,1)}, u32[]{:S(2)}) copy-start(bf16[1,128,1536]{2,1,0:T(8,128)(2,1)} %param.21) | copy-start | bytes 1179652
  93.6 37.8 %all-to-all-start.1 = ((bf16[128,2,768]{2,1,0:T(2,128)(2,1)}), bf16[128,2,768]{2,1,0:T(2,128)(2,1)S(1)}, u32[]{:S(2)}, u32[]{:S(2)}) async-start(bf16[128,2,768]{2,1,0:T(2,128)(2,1)} %reshape.255), calls=%async_computation.1 | async-start | bytes 786432 | tf_op jit(solution)/shard_map/all_to_all | solution.py:100
  110.9 9.5 %collective-permute-start = (bf16[1,128,32]{2,1,0:T(8,128)(2,1)S(1)}, bf16[1,128,32]{2,1,0:T(8,128)(2,1)S(1)}, u32[]{:S(2)}, u32[]{:S(2)}) collective-permute-start(bf16[1,128,32]{2,1,0:T(8,128)(2,1)S(1)} %get-tuple-element.104), channel_id=1, source_target_pairs={{0,1},{1,2},{2,3},{3,0},{4,5},{5,6},{6,7},{7,4},{8,9},{9,10},{10,1... | collective-permute-start | bytes 24584 | tf_op jit(solution)/shard_map/ppermute | solution.py:32
  113.0 9.7 %collective-permute-start.1 = (bf16[1,128,32]{2,1,0:T(8,128)(2,1)S(1)}, bf16[1,128,32]{2,1,0:T(8,128)(2,1)S(1)}, u32[]{:S(2)}, u32[]{:S(2)}) collective-permute-start(bf16[1,128,32]{2,1,0:T(8,128)(2,1)S(1)} %get-tuple-element.103), channel_id=1, source_target_pairs={{1,0},{2,1},{3,2},{0,3},{5,4},{6,5},{7,6},{4,7},{9,8},{10,9},{11,1... | collective-permute-start | bytes 24584 | tf_op jit(solution)/shard_map/ppermute | solution.py:35
  201.1 14.0 %copy-start.2 = (bf16[128,1536]{1,0:T(8,128)(2,1)}, bf16[128,1536]{1,0:T(8,128)(2,1)S(1)}, u32[]{:S(2)}) copy-start(bf16[128,1536]{1,0:T(8,128)(2,1)S(1)} %get-tuple-element.231) | copy-start | bytes 1179652
  211.8 3.3 %copy-start.4 = (f32[1,4,16]{2,1,0:T(4,128)}, f32[1,4,16]{2,1,0:T(4,128)S(1)}, u32[]{:S(2)}) copy-start(f32[1,4,16]{2,1,0:T(4,128)S(1)} %psum.7) | copy-start | bytes 772
where the time goes:
time: 216 us; the launch traced here: 215 us
  local copies, waits for them, and re-layouts  62.1 us (29%)
  blocking collectives  53.9 us (25%)
  loops' own time  31.9 us (15%)
  starting transfers between devices  25 us (12%)
  matrix products  15 us (7%)
  other arithmetic  12.6 us (6%)
  waiting for transfers between devices  10.5 us (5%)
  between operations  4.12 us (2%)
    all_to_all x1, blocking collectives, summed_on_arrival(): parts = lax.all_to_all(split_up(value, dim, peers), axis, 0, 0, tiled=True)  44 us
    another operation x1, loops' own time, correlate_one(): gramians = lax.map(one_lag, offsets)  31.6 us
    dynamic_update_slice x16, local copies, waits for them, and re-layouts, correlate_one(): gramians = lax.map(one_lag, offsets)  23.1 us
    all_to_all x1, starting transfers between devices, local(): lax.all_to_all(summed, 'slab', split_axis=0, concat_axis=1, tiled=True)  17.2 us
    psum x1, blocking collectives, local(): totals = lax.psum(search_regions, 'col')  9.86 us
    dynamic_slice x16, local copies, waits for them, and re-layouts, correlate_one(): gramians = lax.map(one_lag, offsets)  9.38 us
    gather x4, local copies, waits for them, and re-layouts, project_block(): lax.dynamic_slice_in_dim(planes, opening, tile_count, 1)  8.96 us
    concatenate x4, other arithmetic, project_block(): doubled = jnp.concatenate([tiled, tiled], axis=2)  8.11 us
  transfers between devices with their start and end apart: 3, of which 3 were waited for; matrix products, arithmetic and copies ran while one was open for 0% of the time, Pallas kernels for 0%

commit v1 on v0

v1 whole, which is shorter than its diff:
```python
import math

import jax
import jax.numpy as jnp
from jax import lax
from jax.experimental import pallas as pl
from jax.experimental.pallas import tpu as pltpu
from jax.sharding import PartitionSpec as P

LAG = 32
WU = 16
LAGZ = 4
WZ = 4
ROWS = 144


def project_kernel(place, owner, shift, cls, weights, bank, volume, *outs_held):
    outs, held = outs_held[:-1], outs_held[-1]
    angles = weights.shape[0]
    columns = volume.shape[1]
    tile = bank.shape[1]
    banks = bank.shape[0]
    tiles = columns // tile
    quarters = len(outs)
    per = tiles // quarters
    lane = lax.broadcasted_iota(jnp.int32, (angles, angles), 1)
    wide = jnp.broadcast_to(owner[...].astype(jnp.float32), (angles, angles))
    picks = wide.T.astype(jnp.int32) == lane
    onehot = picks.astype(jnp.float32)
    shifts = jnp.sum(onehot * shift[...].astype(jnp.float32), axis=1, keepdims=True)
    classes = jnp.sum(onehot * cls[...].astype(jnp.float32), axis=1, keepdims=True)
    shifts = shifts.astype(jnp.int32) + (tiles - per * place[0])
    shifts = jnp.where(shifts >= tiles, shifts - tiles, shifts)
    chosen = jnp.dot(
        onehot.astype(jnp.bfloat16), weights[...], preferred_element_type=jnp.float32
    ).astype(jnp.bfloat16)
    classes = jnp.broadcast_to(classes, (angles, tile)).astype(jnp.int32)
    masks = [(classes == c).astype(jnp.bfloat16) for c in range(banks)]
    stacked = bank[...].reshape(banks * tile, tile)
    width = 4 * tile
    for j in range(columns // width):
        ray = jnp.dot(
            chosen, volume[:, j * width : (j + 1) * width], preferred_element_type=jnp.float32
        ).astype(jnp.bfloat16)
        for t in range(width // tile):
            piece = ray[:, t * tile : (t + 1) * tile]
            spreadable = jnp.concatenate([piece * m for m in masks], axis=1)
            at = j * width + t * tile
            held[:, at : at + tile] = jnp.dot(
                spreadable, stacked, preferred_element_type=jnp.float32
            )
    group = 8
    bits = (tiles - 1).bit_length()
    for g in range(angles // group):
        rows = slice(g * group, (g + 1) * group)
        amount = jnp.broadcast_to(shifts[rows], (group, tile))
        parts = [held[rows, t * tile : (t + 1) * tile] for t in range(tiles)]
        for b in range(bits):
            keep = ((amount >> b) & 1) == 0
            parts = [
                jnp.where(keep, parts[t], parts[(t - (1 << b)) % tiles]) for t in range(tiles)
            ]
        for t in range(tiles):
            q, c = divmod(t, per)
            outs[q][rows, c * tile : (c + 1) * tile] = parts[t].astype(jnp.bfloat16)


def project(place, owner, shift, cls, weights, bank, volume, quarters):
    angles = weights.shape[0]
    columns = volume.shape[1]
    return pl.pallas_call(
        project_kernel,
        out_shape=[jax.ShapeDtypeStruct((angles, columns // quarters), jnp.bfloat16)] * quarters,
        in_specs=[pl.BlockSpec(memory_space=pltpu.SMEM)]
        + [pl.BlockSpec(memory_space=pltpu.VMEM)] * 6,
        scratch_shapes=[pltpu.VMEM((angles, columns), jnp.float32)],
        name="project",
    )(place, owner[None], shift[None], cls[None], weights, bank, volume)


def correlate_kernel(starts, owned, across, out):
    slices, columns = owned.shape
    tile = 128
    tiles = columns // tile
    start_slice = starts[0]
    first = starts[1] + LAG
    pieces = []
    for a in range(WZ):
        turn = lax.rem(2 * slices - start_slice - a, slices)
        row = []
        for t in range(tiles):
            block = across[pl.ds(first + t * tile, ROWS), :]
            row.append(pltpu.roll(block, turn, 1).astype(jnp.bfloat16))
        pieces.append(jnp.concatenate(row, axis=1))
    lhs = jnp.concatenate(pieces, axis=0)
    rhs = jnp.concatenate(
        [owned[:, t * tile : (t + 1) * tile] for t in range(tiles)], axis=0
    )
    sums = jnp.dot(lhs, rhs, preferred_element_type=jnp.float32)
    lanes = lax.broadcasted_iota(jnp.int32, (8, tile), 1)
    subs = lax.broadcasted_iota(jnp.int32, (8, tile), 0)
    results = []
    for a in range(WZ):
        total = jnp.zeros((8, tile), jnp.float32)
        for i in range(ROWS // 8):
            block = sums[a * ROWS + i * 8 : a * ROWS + i * 8 + 8]
            if i < WU // 8:
                block = jnp.where(lanes < tile // 2, block, 0.0)
            if i >= tile // 8:
                block = jnp.where(lanes >= tile // 2, block, 0.0)
            total = total + pltpu.roll(block, (-8 * i) % tile, 1)
        aligned = jnp.zeros((8, tile), jnp.float32)
        for d in range(WU):
            here = ((subs - d) & (tile - 1)) == lanes
            value = jnp.sum(jnp.where(here, total, 0.0))
            aligned = jnp.where(lanes == d, value, aligned)
        results.append(aligned[0:1])
    results.append(jnp.zeros((8 - WZ, tile), jnp.float32))
    out[...] = jnp.concatenate(results, axis=0)


def correlate(starts, owned, across):
    return pl.pallas_call(
        correlate_kernel,
        out_shape=jax.ShapeDtypeStruct((8, 128), jnp.float32),
        in_specs=[
            pl.BlockSpec(memory_space=pltpu.SMEM),
            pl.BlockSpec(memory_space=pltpu.VMEM),
            pl.BlockSpec(memory_space=pltpu.VMEM),
        ],
        name="correlate",
    )(starts, owned, across)


def local(
    volume,
    detector_row_weight,
    tile_bank,
    tile_class,
    tile_shift,
    owner_angle,
    measured,
    window_slice,
    window_col,
):
    count = lax.axis_size("col")
    place = lax.axis_index("col").astype(jnp.int32)[None]
    ring = [[(i, (i + d) % count) for i in range(count)] for d in range(count)]
    pieces = project(
        place, owner_angle, tile_shift, tile_class, detector_row_weight, tile_bank, volume[0], count
    )
    total = pieces[0].astype(jnp.float32)
    for d in range(1, count):
        total = total + lax.ppermute(pieces[d], "col", ring[d]).astype(jnp.float32)
    summed = total.astype(jnp.bfloat16)[:, None, :]
    owned = lax.all_to_all(summed, "slab", split_axis=0, concat_axis=1, tiled=True)
    seen = measured[0]
    slices, quarter = seen.shape
    low = lax.ppermute(seen[:, quarter - LAG :], "col", ring[1])
    high = lax.ppermute(seen[:, :LAG], "col", ring[count - 1])
    rest = jnp.zeros((128 - 2 * LAG, slices), jnp.bfloat16)
    across = jnp.concatenate([low.T, seen.T, high.T, rest], axis=0).astype(jnp.float32)
    starts = jnp.concatenate([window_slice, window_col])
    part = correlate(starts, owned[0], across)[None, :WZ, :WU]
    norm_factor = 1.0 / math.sqrt(slices * quarter * count)
    totals = lax.psum(part * norm_factor, "col")
    lag_slices = jnp.arange(WZ, dtype=jnp.int32)
    lag_columns = jnp.arange(WU, dtype=jnp.int32)
    weight_grid = totals * totals
    along_slices = (window_slice[:, None] + lag_slices[None, :]).astype(jnp.float32) / LAGZ
    along_columns = (window_col[:, None] + lag_columns[None, :]).astype(jnp.float32) / LAG
    denominator = jnp.mean(weight_grid, axis=(1, 2)) + 1e-06
    shift_slices = jnp.mean(weight_grid * along_slices[:, :, None], axis=(1, 2)) / denominator
    shift_columns = jnp.mean(weight_grid * along_columns[:, None, :], axis=(1, 2)) / denominator
    return (owned, totals, jnp.stack([shift_slices, shift_columns]))


def solution(mesh):
    return jax.shard_map(
        local,
        mesh=mesh,
        in_specs=(
            P("slab", "col", None),
            P(None, "col"),
            P(),
            P(),
            P(),
            P(),
            P("slab", None, "col"),
            P("slab"),
            P("slab"),
        ),
        out_specs=(P("slab", None, "col"), P("slab", None, None), P(None, "slab")),
        check_vma=False,
    )
```

time: 216 us -> 110 us (0.51)
  the two profiles are of different devices: /device:TPU:2 before, /device:TPU:8 now
where the time goes in v1:
time: 110 us
  starting transfers between devices  37.8 us (34%)
  waiting for transfers between devices  31.2 us (28%)
  blocking collectives  18.2 us (17%)
  Pallas kernels  9.96 us (9%)
  other arithmetic  5.89 us (5%)
  between operations  4.03 us (4%)
  local copies, waits for them, and re-layouts  2.77 us (3%)
    all_to_all x1, waiting for transfers between devices, local(): lax.all_to_all(summed, 'slab', split_axis=0, concat_axis=1, tiled=True)  18.9 us
    psum x1, blocking collectives, local(): totals = lax.psum(part * norm_factor, 'col')  18.2 us
    all_to_all x1, starting transfers between devices, local(): lax.all_to_all(summed, 'slab', split_axis=0, concat_axis=1, tiled=True)  17.4 us
    ppermute x3, starting transfers between devices, local(): total = total + lax.ppermute(pieces[d], 'col', ring[d]).astype(jnp.float32)  12.8 us
    ppermute x3, waiting for transfers between devices, local(): total = total + lax.ppermute(pieces[d], 'col', ring[d]).astype(jnp.float32)  12.3 us
    pallas_call x1, Pallas kernels, project(): pl.pallas_call(project_kernel, out_shape=[jax.ShapeDtypeStruct((angles, c...  6.98 us
    ppermute x1, starting transfers between devices, local(): high = lax.ppermute(seen[:, :LAG], 'col', ring[count - 1])  4.25 us
    ppermute x1, starting transfers between devices, local(): low = lax.ppermute(seen[:, quarter - LAG:], 'col', ring[1])  3.4 us
  transfers between devices with their start and end apart: 6, of which 2 were waited for; matrix products, arithmetic and copies ran while one was open for 5% of the time, Pallas kernels for 0%

profile of v1, /device:TPU:8, one launch (start us, length us, event | category | flops | bytes accessed | tf_op | source)
XLA Modules:
  0.0 109.9 jit_solution(5638851018183800606)
XLA Ops:
  0.6 7.0 %project.1 = (bf16[128,1536]{1,0:T(8,128)(2,1)}, bf16[128,1536]{1,0:T(8,128)(2,1)}, bf16[128,1536]{1,0:T(8,128)(2,1)}, bf16[128,1536]{1,0:T(8,128)(2,1)}) custom-call(s32[1]{0:T(128)} %bitcast.place, s32[1,128]{1,0:T(1,128)} %bitcast.32, s32[1,128]{1,0:T(1,128)} %bitcast.33, s32[1,128]{1,0:T(1,128)} %bitcast.34, bf16[128,128]{1,0:T(8,128)(2,1)} %weights.1, ...), custom_call_target="tpu_custom_call" | custom-call | tf_op jit(solution)/shard_map/project/pallas_call | solution.py:71
  7.6 4.3 %collective-permute-start = (bf16[128,1536]{1,0:T(8,128)(2,1)}, bf16[128,1536]{1,0:T(8,128)(2,1)S(1)}, u32[]{:S(2)}, u32[]{:S(2)}) collective-permute-start(bf16[128,1536]{1,0:T(8,128)(2,1)} %get-tuple-element.8), channel_id=1, source_target_pairs={{0,1},{1,2},{2,3},{3,0},{4,5},{5,6},{6,7},{7,4},{8,9},{9,10},{10,1... | collective-permute-start | bytes 1179656 | tf_op jit(solution)/shard_map/ppermute | solution.py:154
  11.9 6.1 %collective-permute-start.1 = (bf16[128,1536]{1,0:T(8,128)(2,1)}, bf16[128,1536]{1,0:T(8,128)(2,1)S(1)}, u32[]{:S(2)}, u32[]{:S(2)}) collective-permute-start(bf16[128,1536]{1,0:T(8,128)(2,1)} %get-tuple-element.9), channel_id=1, source_target_pairs={{0,2},{1,3},{2,0},{3,1},{4,6},{5,7},{6,4},{7,5},{8,10},{9,11},{10,... | collective-permute-start | bytes 1179656 | tf_op jit(solution)/shard_map/ppermute | solution.py:154
  18.0 2.4 %collective-permute-start.2 = (bf16[128,1536]{1,0:T(8,128)(2,1)}, bf16[128,1536]{1,0:T(8,128)(2,1)S(1)}, u32[]{:S(2)}, u32[]{:S(2)}) collective-permute-start(bf16[128,1536]{1,0:T(8,128)(2,1)} %get-tuple-element.10), channel_id=1, source_target_pairs={{0,3},{1,0},{2,1},{3,2},{4,7},{5,4},{6,5},{7,6},{8,11},{9,8},{10,9... | collective-permute-start | bytes 1179656 | tf_op jit(solution)/shard_map/ppermute | solution.py:154
  20.5 0.2 copy.16
  20.7 3.4 %collective-permute-start.3 = (bf16[128,32]{0,1:T(8,128)(2,1)S(1)}, bf16[128,32]{0,1:T(8,128)(2,1)S(1)}, u32[]{:S(2)}, u32[]{:S(2)}) collective-permute-start(bf16[128,32]{0,1:T(8,128)(2,1)S(1)} %get-tuple-element.16), channel_id=1, source_target_pairs={{0,1},{1,2},{2,3},{3,0},{4,5},{5,6},{6,7},{7,4},{8,9},{9,10},{10,1... | collective-permute-start | bytes 24584 | tf_op jit(solution)/shard_map/ppermute | solution.py:159
  24.1 4.2 %collective-permute-start.4 = (bf16[128,32]{0,1:T(8,128)(2,1)S(1)}, bf16[128,32]{0,1:T(8,128)(2,1)S(1)}, u32[]{:S(2)}, u32[]{:S(2)}) collective-permute-start(bf16[128,32]{0,1:T(8,128)(2,1)S(1)} %get-tuple-element.17), channel_id=1, source_target_pairs={{0,3},{1,0},{2,1},{3,2},{4,7},{5,4},{6,5},{7,6},{8,11},{9,8},{10,9... | collective-permute-start | bytes 24584 | tf_op jit(solution)/shard_map/ppermute | solution.py:160
  29.7 12.3 %collective-permute-done.1 = bf16[128,1536]{1,0:T(8,128)(2,1)S(1)} collective-permute-done((bf16[128,1536]{1,0:T(8,128)(2,1)}, bf16[128,1536]{1,0:T(8,128)(2,1)S(1)}, u32[]{:S(2)}, u32[]{:S(2)}) %collective-permute-start.1) | collective-permute-done | bytes 393248 | tf_op jit(solution)/shard_map/ppermute | solution.py:154
  42.0 1.2 %fusion = bf16[128,1,1536]{2,0,1:T(8,128)(2,1)S(1)} fusion(bf16[128,1536]{1,0:T(8,128)(2,1)S(1)} %collective-permute-done.2, bf16[128,1536]{1,0:T(8,128)(2,1)S(1)} %collective-permute-done.1, bf16[128,1536]{1,0:T(8,128)(2,1)S(1)} %collective-permute-done, bf16[128,1536]{1,0:T(8,128)(2,1)} %get-tuple-element.7), kind=kLoop, calls=%fused_computation.2 | loop fusion | flops 1572864 | bytes 1966080 | tf_op jit(solution)/shard_map/broadcast_in_dim | solution.py:155
  43.2 0.5 broadcast.43
  43.7 0.9 reduce.3
  44.6 0.8 reshape.56
  45.4 17.4 %all-to-all-start = ((bf16[128,2,768]{2,1,0:T(2,128)(2,1)}), bf16[128,2,768]{2,1,0:T(2,128)(2,1)S(1)}, u32[]{:S(2)}, u32[]{:S(2)}) async-start(bf16[128,2,768]{2,1,0:T(2,128)(2,1)} %reshape.56), calls=%async_computation | async-start | bytes 786432 | tf_op jit(solution)/shard_map/all_to_all | solution.py:156
  62.8 0.6 pad_add_fusion.starts
  63.4 0.1 pad.5.clone
  63.5 1.2 %maximum_convert_fusion.across = f32[1664,128]{1,0:T(8,128)} fusion(bf16[32,128]{1,0:T(8,128)(2,1)S(1)} %bitcast.31, bf16[1536,128]{1,0:T(8,128)(2,1)S(1)} %bitcast.26, bf16[32,128]{1,0:T(8,128)(2,1)S(1)} %bitcast.30, bf16[1664]{0:T(1024)(128)(2,1)S(1)} %pad.5.clone), kind=kLoop, calls=%fused_computation.1 | loop fusion | flops 1703936 | bytes 1264896 | tf_op jit(solution)/shard_map/convert_element_type | solution.py:162
  64.7 18.9 %all-to-all-done = bf16[128,2,768]{2,1,0:T(2,128)(2,1)S(1)} async-done(((bf16[128,2,768]{2,1,0:T(2,128)(2,1)}), bf16[128,2,768]{2,1,0:T(2,128)(2,1)S(1)}, u32[]{:S(2)}, u32[]{:S(2)}) %all-to-all-start) | async-done | bytes 393248 | tf_op jit(solution)/shard_map/all_to_all | solution.py:156
  83.6 0.3 reshape.57
  83.9 0.8 copy.21
  84.7 3.0 %correlate.1 = f32[8,128]{1,0:T(8,128)} custom-call(s32[2]{0:T(128)} %pad_add_fusion.starts, bf16[128,1536]{1,0:T(8,128)(2,1)} %bitcast.28, f32[1664,128]{1,0:T(8,128)} %maximum_convert_fusion.across), custom_call_target="tpu_custom_call" | custom-call | tf_op jit(solution)/shard_map/correlate/pallas_call | solution.py:123
  87.7 0.7 multiply_bitcast_fusion
  88.4 18.2 %psum.7 = f32[1,4,16]{2,1,0:T(4,128)S(1)} all-reduce(f32[1,4,16]{2,1,0:T(4,128)S(1)} %multiply_bitcast_fusion), channel_id=1, replica_groups=mesh['slab'=128,'col'=4] {'col'}, use_global_device_ids=true, to_apply=%region_0.0 | all-reduce | flops 64 | bytes 512 | tf_op jit(solution)/shard_map/psum | solution.py:166
  106.6 0.8 multiply_reduce_fusion.1
  109.3 0.6 pad_maximum_fusion
  (12 shorter events, 0.0 us)
Async XLA Ops:
  0.6 19.8 %copy-start = (bf16[1,128,1536]{2,1,0:T(8,128)(2,1)S(1)}, bf16[1,128,1536]{2,1,0:T(8,128)(2,1)}, u32[]{:S(2)}) copy-start(bf16[1,128,1536]{2,1,0:T(8,128)(2,1)} %param.15) | copy-start | bytes 1179652
  7.6 22.0 %collective-permute-start = (bf16[128,1536]{1,0:T(8,128)(2,1)}, bf16[128,1536]{1,0:T(8,128)(2,1)S(1)}, u32[]{:S(2)}, u32[]{:S(2)}) collective-permute-start(bf16[128,1536]{1,0:T(8,128)(2,1)} %get-tuple-element.8), channel_id=1, source_target_pairs={{0,1},{1,2},{2,3},{3,0},{4,5},{5,6},{6,7},{7,4},{8,9},{9,10},{10,1... | collective-permute-start | bytes 1179656 | tf_op jit(solution)/shard_map/ppermute | solution.py:154
  11.9 30.1 %collective-permute-start.1 = (bf16[128,1536]{1,0:T(8,128)(2,1)}, bf16[128,1536]{1,0:T(8,128)(2,1)S(1)}, u32[]{:S(2)}, u32[]{:S(2)}) collective-permute-start(bf16[128,1536]{1,0:T(8,128)(2,1)} %get-tuple-element.9), channel_id=1, source_target_pairs={{0,2},{1,3},{2,0},{3,1},{4,6},{5,7},{6,4},{7,5},{8,10},{9,11},{10,... | collective-permute-start | bytes 1179656 | tf_op jit(solution)/shard_map/ppermute | solution.py:154
  18.0 23.9 %collective-permute-start.2 = (bf16[128,1536]{1,0:T(8,128)(2,1)}, bf16[128,1536]{1,0:T(8,128)(2,1)S(1)}, u32[]{:S(2)}, u32[]{:S(2)}) collective-permute-start(bf16[128,1536]{1,0:T(8,128)(2,1)} %get-tuple-element.10), channel_id=1, source_target_pairs={{0,3},{1,0},{2,1},{3,2},{4,7},{5,4},{6,5},{7,6},{8,11},{9,8},{10,9... | collective-permute-start | bytes 1179656 | tf_op jit(solution)/shard_map/ppermute | solution.py:154
  20.7 42.7 %collective-permute-start.3 = (bf16[128,32]{0,1:T(8,128)(2,1)S(1)}, bf16[128,32]{0,1:T(8,128)(2,1)S(1)}, u32[]{:S(2)}, u32[]{:S(2)}) collective-permute-start(bf16[128,32]{0,1:T(8,128)(2,1)S(1)} %get-tuple-element.16), channel_id=1, source_target_pairs={{0,1},{1,2},{2,3},{3,0},{4,5},{5,6},{6,7},{7,4},{8,9},{9,10},{10,1... | collective-permute-start | bytes 24584 | tf_op jit(solution)/shard_map/ppermute | solution.py:159
  24.1 39.3 %collective-permute-start.4 = (bf16[128,32]{0,1:T(8,128)(2,1)S(1)}, bf16[128,32]{0,1:T(8,128)(2,1)S(1)}, u32[]{:S(2)}, u32[]{:S(2)}) collective-permute-start(bf16[128,32]{0,1:T(8,128)(2,1)S(1)} %get-tuple-element.17), channel_id=1, source_target_pairs={{0,3},{1,0},{2,1},{3,2},{4,7},{5,4},{6,5},{7,6},{8,11},{9,8},{10,9... | collective-permute-start | bytes 24584 | tf_op jit(solution)/shard_map/ppermute | solution.py:160
  45.4 38.2 %all-to-all-start = ((bf16[128,2,768]{2,1,0:T(2,128)(2,1)}), bf16[128,2,768]{2,1,0:T(2,128)(2,1)S(1)}, u32[]{:S(2)}, u32[]{:S(2)}) async-start(bf16[128,2,768]{2,1,0:T(2,128)(2,1)} %reshape.56), calls=%async_computation | async-start | bytes 786432 | tf_op jit(solution)/shard_map/all_to_all | solution.py:156
  106.6 3.3 %copy-start.1 = (f32[1,4,16]{2,1,0:T(4,128)}, f32[1,4,16]{2,1,0:T(4,128)S(1)}, u32[]{:S(2)}) copy-start(f32[1,4,16]{2,1,0:T(4,128)S(1)} %psum.7) | copy-start | bytes 772

commit v2 on v1

--- a/solution.py
+++ b/solution.py
@@ -14,23 +14,25 @@
 ROWS = 144
 
 
-def project_kernel(place, owner, shift, cls, weights, bank, volume, *outs_held):
-    outs, held = outs_held[:-1], outs_held[-1]
+def project_kernel(owner, shift, cls, weights, bank, volume, out, held):
     angles = weights.shape[0]
     columns = volume.shape[1]
     tile = bank.shape[1]
     banks = bank.shape[0]
     tiles = columns // tile
-    quarters = len(outs)
+    planes = out.shape[1]
+    kinds = angles // planes
+    quarters = out.shape[0] // kinds
     per = tiles // quarters
     lane = lax.broadcasted_iota(jnp.int32, (angles, angles), 1)
+    row = lax.broadcasted_iota(jnp.int32, (angles, angles), 0)
+    order = ((row % planes) * kinds + row // planes == lane).astype(jnp.bfloat16)
     wide = jnp.broadcast_to(owner[...].astype(jnp.float32), (angles, angles))
-    picks = wide.T.astype(jnp.int32) == lane
-    onehot = picks.astype(jnp.float32)
+    picks = (wide.T.astype(jnp.int32) == lane).astype(jnp.bfloat16)
+    onehot = jnp.dot(order, picks, preferred_element_type=jnp.float32)
     shifts = jnp.sum(onehot * shift[...].astype(jnp.float32), axis=1, keepdims=True)
     classes = jnp.sum(onehot * cls[...].astype(jnp.float32), axis=1, keepdims=True)
-    shifts = shifts.astype(jnp.int32) + (tiles - per * place[0])
-    shifts = jnp.where(shifts >= tiles, shifts - tiles, shifts)
+    shifts = shifts.astype(jnp.int32)
     chosen = jnp.dot(
         onehot.astype(jnp.bfloat16), weights[...], preferred_element_type=jnp.float32
     ).astype(jnp.bfloat16)
@@ -60,22 +62,26 @@
             parts = [
                 jnp.where(keep, parts[t], parts[(t - (1 << b)) % tiles]) for t in range(tiles)
             ]
+        kind, plane = divmod(g * group, planes)
+        high, low = divmod(kind, 2)
         for t in range(tiles):
             q, c = divmod(t, per)
-            outs[q][rows, c * tile : (c + 1) * tile] = parts[t].astype(jnp.bfloat16)
-
-
-def project(place, owner, shift, cls, weights, bank, volume, quarters):
+            out[(high * quarters + q) * 2 + low, plane : plane + group, c * tile : (c + 1) * tile] = (
+                parts[t].astype(jnp.bfloat16)
+            )
+
+
+def project(owner, shift, cls, weights, bank, volume, quarters, kinds):
     angles = weights.shape[0]
     columns = volume.shape[1]
     return pl.pallas_call(
         project_kernel,
-        out_shape=[jax.ShapeDtypeStruct((angles, columns // quarters), jnp.bfloat16)] * quarters,
-        in_specs=[pl.BlockSpec(memory_space=pltpu.SMEM)]
-        + [pl.BlockSpec(memory_space=pltpu.VMEM)] * 6,
+        out_shape=jax.ShapeDtypeStruct(
+            (quarters * kinds, angles // kinds, columns // quarters), jnp.bfloat16
+        ),
         scratch_shapes=[pltpu.VMEM((angles, columns), jnp.float32)],
         name="project",
-    )(place, owner[None], shift[None], cls[None], weights, bank, volume)
+    )(owner[None], shift[None], cls[None], weights, bank, volume)
 
 
 def correlate_kernel(starts, owned, across, out):
@@ -143,27 +149,31 @@
     window_slice,
     window_col,
 ):
-    count = lax.axis_size("col")
-    place = lax.axis_index("col").astype(jnp.int32)[None]
+    count = lax.axis_size("zl")
+    halves = lax.axis_size("zh")
+    cores = lax.axis_size("co")
+    kinds = halves * cores
     ring = [[(i, (i + d) % count) for i in range(count)] for d in range(count)]
     pieces = project(
-        place, owner_angle, tile_shift, tile_class, detector_row_weight, tile_bank, volume[0], count
-    )
-    total = pieces[0].astype(jnp.float32)
-    for d in range(1, count):
-        total = total + lax.ppermute(pieces[d], "col", ring[d]).astype(jnp.float32)
-    summed = total.astype(jnp.bfloat16)[:, None, :]
-    owned = lax.all_to_all(summed, "slab", split_axis=0, concat_axis=1, tiled=True)
+        owner_angle, tile_shift, tile_class, detector_row_weight, tile_bank, volume[0], count, kinds
+    )
+    parts = lax.all_to_all(pieces, ("zh", "zl", "co"), 0, 0, tiled=True)
+    planes, quarter = parts.shape[1:]
+    parts = parts.reshape(halves, count, cores, planes, quarter)
+    summed = jnp.sum(parts.astype(jnp.float32), axis=1).astype(jnp.bfloat16)
+    summed = jnp.transpose(summed.reshape(kinds, planes, quarter), (1, 0, 2))
+    owned = lax.all_to_all(summed, ("y", "x"), 0, 0, tiled=True)
+    owned = owned.reshape(1, planes * kinds, quarter)
     seen = measured[0]
     slices, quarter = seen.shape
-    low = lax.ppermute(seen[:, quarter - LAG :], "col", ring[1])
-    high = lax.ppermute(seen[:, :LAG], "col", ring[count - 1])
+    low = lax.ppermute(seen[:, quarter - LAG :], "zl", ring[1])
+    high = lax.ppermute(seen[:, :LAG], "zl", ring[count - 1])
     rest = jnp.zeros((128 - 2 * LAG, slices), jnp.bfloat16)
     across = jnp.concatenate([low.T, seen.T, high.T, rest], axis=0).astype(jnp.float32)
     starts = jnp.concatenate([window_slice, window_col])
     part = correlate(starts, owned[0], across)[None, :WZ, :WU]
     norm_factor = 1.0 / math.sqrt(slices * quarter * count)
-    totals = lax.psum(part * norm_factor, "col")
+    totals = lax.psum(part * norm_factor, "zl")
     lag_slices = jnp.arange(WZ, dtype=jnp.int32)
     lag_columns = jnp.arange(WU, dtype=jnp.int32)
     weight_grid = totals * totals
@@ -176,20 +186,27 @@
 
 
 def solution(mesh):
+    slab, col = mesh.axis_names
+    cols = mesh.shape[col]
+    rows = mesh.shape[slab]
+    parts = jax.sharding.Mesh(
+        mesh.devices.reshape(rows // 16, 4, 2, 2, cols), ("y", "x", "zh", "co", "zl")
+    )
+    slab = ("y", "x", "zh", "co")
     return jax.shard_map(
         local,
-        mesh=mesh,
+        mesh=parts,
         in_specs=(
-            P("slab", "col", None),
-            P(None, "col"),
-            P(),
-            P(),
-            P(),
-            P(),
-            P("slab", None, "col"),
-            P("slab"),
-            P("slab"),
+            P(slab, "zl", None),
+            P(None, "zl"),
+            P(),
+            P(),
+            P(),
+            P(),
+            P(slab, None, "zl"),
+            P(slab),
+            P(slab),
         ),
-        out_specs=(P("slab", None, "col"), P("slab", None, None), P(None, "slab")),
+        out_specs=(P(slab, None, "zl"), P(slab, None, None), P(None, slab)),
         check_vma=False,
     )

time: 110 us -> 103 us (0.936)
  waiting for transfers between devices: 31.2 us -> 42.2 us
  starting transfers between devices: 37.8 us -> 28.3 us
  blocking collectives: 18.2 us -> 11.2 us
  other arithmetic: 5.89 us -> 4.11 us
    all_to_all x1 -> x2, waiting for transfers between devices: 18.9 us -> 42.2 us  [the longest x1 28.7 us: local(): parts = lax.all_to_all(pieces, ('zh', 'zl', 'co'), 0, 0, tiled=True)]
    ppermute x5 -> x2, starting transfers between devices: 20.5 us -> 7.55 us  [the longest x1 5.63 us: local(): high = lax.ppermute(seen[:, :LAG], 'zl', ring[count - 1])]
    ppermute x5 -> x2, waiting for transfers between devices: 12.3 us -> 0.01 us  [the longest x1 0.01 us: local(): high = lax.ppermute(seen[:, :LAG], 'zl', ring[count - 1])]
    psum x1, blocking collectives: 18.2 us -> 11.2 us  [local(): totals = lax.psum(part * norm_factor, 'zl')]
    all_to_all x1 -> x2, starting transfers between devices: 17.4 us -> 20.7 us  [the longest x1 10.5 us: local(): parts = lax.all_to_all(pieces, ('zh', 'zl', 'co'), 0, 0, tiled=True)]
    broadcast_in_dim x2 -> x0, other arithmetic: 2.09 us -> none  [local(): summed = total.astype(jnp.bfloat16)[:, None, :]]
    unnamed x8 -> x5, local copies, waits for them, and re-layouts: 2.18 us -> 0.23 us
    reshape x0 -> x2, local copies, waits for them, and re-layouts: none -> 1.89 us  [the longest x1 1.05 us: local(): summed = jnp.transpose(summed.reshape(kinds, planes, quarter), (1, 0, 2))]
  transfers between devices with their start and end apart: 6 -> 4, of which waited for: 2 -> 2; matrix products, arithmetic and copies ran while one was open for 5% -> 3% of each run, Pallas kernels for 0% -> 0%
where the time goes in v2:
time: 103 us
  waiting for transfers between devices  42.2 us (41%)
  starting transfers between devices  28.3 us (27%)
  blocking collectives  11.2 us (11%)
  Pallas kernels  10.1 us (10%)
  other arithmetic  4.11 us (4%)
  between operations  4.07 us (4%)
  local copies, waits for them, and re-layouts  3.03 us (3%)
    all_to_all x1, waiting for transfers between devices, local(): parts = lax.all_to_all(pieces, ('zh', 'zl', 'co'), 0, 0, tiled=True)  28.7 us
    all_to_all x1, waiting for transfers between devices, local(): owned = lax.all_to_all(summed, ('y', 'x'), 0, 0, tiled=True)  13.5 us
    psum x1, blocking collectives, local(): totals = lax.psum(part * norm_factor, 'zl')  11.2 us
    all_to_all x1, starting transfers between devices, local(): parts = lax.all_to_all(pieces, ('zh', 'zl', 'co'), 0, 0, tiled=True)  10.5 us
    all_to_all x1, starting transfers between devices, local(): owned = lax.all_to_all(summed, ('y', 'x'), 0, 0, tiled=True)  10.2 us
    pallas_call x1, Pallas kernels, project(): pl.pallas_call(project_kernel, out_shape=jax.ShapeDtypeStruct((quarters *...  7.09 us
    ppermute x1, starting transfers between devices, local(): high = lax.ppermute(seen[:, :LAG], 'zl', ring[count - 1])  5.63 us
    pallas_call x1, Pallas kernels, correlate(): pl.pallas_call(correlate_kernel, out_shape=jax.ShapeDtypeStruct((8, 128),...  2.97 us
  transfers between devices with their start and end apart: 4, of which 2 were waited for; matrix products, arithmetic and copies ran while one was open for 3% of the time, Pallas kernels for 0%

profile of v2, /device:TPU:8, one launch (start us, length us, event | category | flops | bytes accessed | tf_op | source)
XLA Modules:
  0.0 103.0 jit_solution(6623042068068082522)
XLA Ops:
  0.6 7.1 %project.1 = bf16[16,32,1536]{2,1,0:T(8,128)(2,1)} custom-call(s32[1,128]{1,0:T(1,128)} %bitcast.29, s32[1,128]{1,0:T(1,128)} %bitcast.30, s32[1,128]{1,0:T(1,128)} %bitcast.31, bf16[128,128]{1,0:T(8,128)(2,1)} %weights.1, bf16[4,128,128]{2,1,0:T(8,128)(2,1)} %bank.1, bf16[128,6144]{1,0:T(8,128)(2,1)} %bitcast.26), custom_call_target="tpu_custom_call" | custom-call | tf_op jit(solution)/shard_map/project/pallas_call | solution.py:77
  7.7 10.5 %all-to-all-start = ((bf16[16,32,1536]{2,1,0:T(8,128)(2,1)}), bf16[16,32,1536]{2,1,0:T(8,128)(2,1)S(1)}, u32[]{:S(2)}, u32[]{:S(2)}) async-start(bf16[16,32,1536]{2,1,0:T(8,128)(2,1)} %project.1), calls=%async_computation | async-start | bytes 3145728 | tf_op jit(solution)/shard_map/all_to_all | solution.py:160
  18.3 0.0 copy-done
  18.3 0.2 copy.14
  18.5 5.6 %collective-permute-start.1 = (bf16[128,32]{0,1:T(8,128)(2,1)S(1)}, bf16[128,32]{0,1:T(8,128)(2,1)S(1)}, u32[]{:S(2)}, u32[]{:S(2)}) collective-permute-start(bf16[128,32]{0,1:T(8,128)(2,1)S(1)} %get-tuple-element.7), channel_id=1, source_target_pairs={{0,3},{1,0},{2,1},{3,2},{4,7},{5,4},{6,5},{7,6},{8,11},{9,8},{10,9... | collective-permute-start | bytes 24584 | tf_op jit(solution)/shard_map/ppermute | solution.py:170
  24.2 1.9 %collective-permute-start = (bf16[128,32]{0,1:T(8,128)(2,1)S(1)}, bf16[128,32]{0,1:T(8,128)(2,1)S(1)}, u32[]{:S(2)}, u32[]{:S(2)}) collective-permute-start(bf16[128,32]{0,1:T(8,128)(2,1)S(1)} %get-tuple-element.6), channel_id=1, source_target_pairs={{0,1},{1,2},{2,3},{3,0},{4,5},{5,6},{6,7},{7,4},{8,9},{9,10},{10,1... | collective-permute-start | bytes 24584 | tf_op jit(solution)/shard_map/ppermute | solution.py:169
  27.4 28.7 %all-to-all-done = bf16[16,32,1536]{2,1,0:T(8,128)(2,1)S(1)} async-done(((bf16[16,32,1536]{2,1,0:T(8,128)(2,1)}), bf16[16,32,1536]{2,1,0:T(8,128)(2,1)S(1)}, u32[]{:S(2)}, u32[]{:S(2)}) %all-to-all-start) | async-done | bytes 1572896 | tf_op jit(solution)/shard_map/all_to_all | solution.py:160
  56.1 0.3 reduce_sum.39
  56.4 1.1 %copy.16 = bf16[4,32,1536]{2,0,1:T(4,128)(2,1)} copy(bf16[4,32,1536]{2,1,0:T(8,128)(2,1)S(1)} %bitcast.25) | data formatting | bytes 786432 | tf_op jit(solution)/shard_map/reshape | solution.py:164
  57.4 10.2 %all-to-all-start.1 = ((bf16[32,4,1536]{2,1,0:T(4,128)(2,1)}), bf16[32,4,1536]{2,1,0:T(4,128)(2,1)S(1)}, u32[]{:S(2)}, u32[]{:S(2)}) async-start(bf16[32,4,1536]{2,1,0:T(4,128)(2,1)} %bitcast.19), calls=%async_computation.1 | async-start | bytes 786432 | tf_op jit(solution)/shard_map/all_to_all | solution.py:165
  67.6 0.6 pad_add_fusion.starts
  68.3 0.1 pad.5.clone
  68.4 0.0 collective-permute-done.1
  68.4 0.0 collective-permute-done
  68.4 1.2 %maximum_convert_fusion.across = f32[1664,128]{1,0:T(8,128)} fusion(bf16[32,128]{1,0:T(8,128)(2,1)S(1)} %bitcast.27, bf16[1536,128]{1,0:T(8,128)(2,1)S(1)} %bitcast.24, bf16[32,128]{1,0:T(8,128)(2,1)S(1)} %bitcast.28, bf16[1664]{0:T(1024)(128)(2,1)S(1)} %pad.5.clone), kind=kLoop, calls=%fused_computation | loop fusion | flops 1703936 | bytes 1264896 | tf_op jit(solution)/shard_map/convert_element_type | solution.py:172
  69.6 13.5 %all-to-all-done.1 = bf16[32,4,1536]{2,1,0:T(4,128)(2,1)S(1)} async-done(((bf16[32,4,1536]{2,1,0:T(4,128)(2,1)}), bf16[32,4,1536]{2,1,0:T(4,128)(2,1)S(1)}, u32[]{:S(2)}, u32[]{:S(2)}) %all-to-all-start.1) | async-done | bytes 393248 | tf_op jit(solution)/shard_map/all_to_all | solution.py:165
  83.0 0.8 squeeze_reshape.3.owned
  83.9 3.0 %correlate.1 = f32[8,128]{1,0:T(8,128)} custom-call(s32[2]{0:T(128)} %pad_add_fusion.starts, bf16[128,1536]{1,0:T(8,128)(2,1)} %squeeze_reshape.3.owned, f32[1664,128]{1,0:T(8,128)} %maximum_convert_fusion.across), custom_call_target="tpu_custom_call" | custom-call | tf_op jit(solution)/shard_map/correlate/pallas_call | solution.py:129
  86.8 0.7 multiply_bitcast_fusion
  87.5 11.2 %psum.7 = f32[1,4,16]{2,1,0:T(4,128)S(1)} all-reduce(f32[1,4,16]{2,1,0:T(4,128)S(1)} %multiply_bitcast_fusion), channel_id=1, replica_groups=mesh['y'=8,'x'=4,'zh'=2,'co'=2,'zl'=4] {'zl'}, use_global_device_ids=true, to_apply=%region_1.0 | all-reduce | flops 64 | bytes 512 | tf_op jit(solution)/shard_map/psum | solution.py:176
  98.7 0.8 multiply_reduce_fusion.1
  101.6 0.6 pad_maximum_fusion
  102.2 0.8 reshape.63
  103.0 0.0 copy-done.1
  (6 shorter events, 0.0 us)
Async XLA Ops:
  7.7 10.6 %copy-start = (bf16[1,128,1536]{2,1,0:T(8,128)(2,1)S(1)}, bf16[1,128,1536]{2,1,0:T(8,128)(2,1)}, u32[]{:S(2)}) copy-start(bf16[1,128,1536]{2,1,0:T(8,128)(2,1)} %param.15) | copy-start | bytes 1179652
  7.7 48.4 %all-to-all-start = ((bf16[16,32,1536]{2,1,0:T(8,128)(2,1)}), bf16[16,32,1536]{2,1,0:T(8,128)(2,1)S(1)}, u32[]{:S(2)}, u32[]{:S(2)}) async-start(bf16[16,32,1536]{2,1,0:T(8,128)(2,1)} %project.1), calls=%async_computation | async-start | bytes 3145728 | tf_op jit(solution)/shard_map/all_to_all | solution.py:160
  18.5 49.8 %collective-permute-start.1 = (bf16[128,32]{0,1:T(8,128)(2,1)S(1)}, bf16[128,32]{0,1:T(8,128)(2,1)S(1)}, u32[]{:S(2)}, u32[]{:S(2)}) collective-permute-start(bf16[128,32]{0,1:T(8,128)(2,1)S(1)} %get-tuple-element.7), channel_id=1, source_target_pairs={{0,3},{1,0},{2,1},{3,2},{4,7},{5,4},{6,5},{7,6},{8,11},{9,8},{10,9... | collective-permute-start | bytes 24584 | tf_op jit(solution)/shard_map/ppermute | solution.py:170
  24.2 44.2 %collective-permute-start = (bf16[128,32]{0,1:T(8,128)(2,1)S(1)}, bf16[128,32]{0,1:T(8,128)(2,1)S(1)}, u32[]{:S(2)}, u32[]{:S(2)}) collective-permute-start(bf16[128,32]{0,1:T(8,128)(2,1)S(1)} %get-tuple-element.6), channel_id=1, source_target_pairs={{0,1},{1,2},{2,3},{3,0},{4,5},{5,6},{6,7},{7,4},{8,9},{9,10},{10,1... | collective-permute-start | bytes 24584 | tf_op jit(solution)/shard_map/ppermute | solution.py:169
  57.4 25.6 %all-to-all-start.1 = ((bf16[32,4,1536]{2,1,0:T(4,128)(2,1)}), bf16[32,4,1536]{2,1,0:T(4,128)(2,1)S(1)}, u32[]{:S(2)}, u32[]{:S(2)}) async-start(bf16[32,4,1536]{2,1,0:T(4,128)(2,1)} %bitcast.19), calls=%async_computation.1 | async-start | bytes 786432 | tf_op jit(solution)/shard_map/all_to_all | solution.py:165
  98.7 4.3 %copy-start.1 = (f32[1,4,16]{2,1,0:T(4,128)}, f32[1,4,16]{2,1,0:T(4,128)S(1)}, u32[]{:S(2)}) copy-start(f32[1,4,16]{2,1,0:T(4,128)S(1)} %psum.7) | copy-start | bytes 772

commit v3 on v2

v3 whole, which is shorter than its diff:
```python
import functools
import math

import jax
import jax.numpy as jnp
from jax import lax
from jax.experimental import pallas as pl
from jax.experimental.pallas import tpu as pltpu
from jax.sharding import PartitionSpec as P

LAG = 32
WU = 16
LAGZ = 4
WZ = 4
ROWS = 144
STEPS = (0, 1, -1, 2, -2, 3, -3)


def project_kernel(place, *refs):
    sources, outs, rest = refs[:6], refs[6:-9], refs[-9:]
    owner, shift, cls, weights, bank, volume, held, ready, sems = rest
    angles = weights.shape[0]
    chunks, _, width = volume.shape
    columns = chunks * width
    tile = bank.shape[1]
    banks = bank.shape[0]
    tiles = columns // tile
    peers, planes = ready.shape[:2]
    halves = angles // planes
    quarters = peers // halves
    per = tiles // quarters
    small = [
        pltpu.make_async_copy(source, target, sems.at[i])
        for i, (source, target) in enumerate(zip(sources[:5], rest[:5]))
    ]
    large = [
        pltpu.make_async_copy(
            sources[5].at[:, j * width : (j + 1) * width], volume.at[j], sems.at[5 + j]
        )
        for j in range(chunks)
    ]
    for copy in small + large:
        copy.start()
    for copy in small:
        copy.wait()
    lane = lax.broadcasted_iota(jnp.int32, (angles, angles), 1)
    row = lax.broadcasted_iota(jnp.int32, (angles, angles), 0)
    slot = row % planes
    order = (slot // 2 * 4 + row // planes * 2 + slot % 2 == lane).astype(jnp.bfloat16)
    wide = jnp.broadcast_to(owner[...].astype(jnp.float32), (angles, angles))
    picks = (wide.T.astype(jnp.int32) == lane).astype(jnp.bfloat16)
    onehot = jnp.dot(order, picks, preferred_element_type=jnp.float32)
    shifts = jnp.sum(onehot * shift[...].astype(jnp.float32), axis=1, keepdims=True)
    classes = jnp.sum(onehot * cls[...].astype(jnp.float32), axis=1, keepdims=True)
    shifts = shifts.astype(jnp.int32)
    chosen = jnp.dot(
        onehot.astype(jnp.bfloat16), weights[...], preferred_element_type=jnp.float32
    ).astype(jnp.bfloat16)
    classes = jnp.broadcast_to(classes, (angles, tile)).astype(jnp.int32)
    masks = [(classes == c).astype(jnp.bfloat16) for c in range(banks)]
    stacked = bank[...].reshape(banks * tile, tile)
    for j in range(chunks):
        large[j].wait()
        ray = jnp.dot(chosen, volume[j], preferred_element_type=jnp.float32).astype(jnp.bfloat16)
        for t in range(width // tile):
            piece = ray[:, t * tile : (t + 1) * tile]
            spreadable = jnp.concatenate([piece * m for m in masks], axis=1)
            at = j * width + t * tile
            held[:, at : at + tile] = jnp.dot(
                spreadable, stacked, preferred_element_type=jnp.float32
            )
    group = 8
    bits = (tiles - 1).bit_length()
    for g in range(angles // group):
        rows = slice(g * group, (g + 1) * group)
        amount = jnp.broadcast_to(shifts[rows], (group, tile))
        parts = [held[rows, t * tile : (t + 1) * tile] for t in range(tiles)]
        for b in range(bits):
            keep = ((amount >> b) & 1) == 0
            parts = [
                jnp.where(keep, parts[t], parts[(t - (1 << b)) % tiles]) for t in range(tiles)
            ]
        high, plane = divmod(g * group, planes)
        for t in range(tiles):
            q, c = divmod(t, per)
            ready[high * quarters + q, plane : plane + group, c * tile : (c + 1) * tile] = parts[
                t
            ].astype(jnp.bfloat16)
    for d in range(peers):
        outs[d][...] = ready[(place[0] + d) & (peers - 1)]


def project(place, owner, shift, cls, weights, bank, volume, quarters, halves):
    angles = weights.shape[0]
    columns = volume.shape[1]
    peers = quarters * halves
    block = (angles // halves, columns // quarters)
    chunks = 8
    small = (owner[None], shift[None], cls[None], weights, bank)
    return pl.pallas_call(
        project_kernel,
        out_shape=[jax.ShapeDtypeStruct(block, jnp.bfloat16)] * peers,
        in_specs=[pl.BlockSpec(memory_space=pltpu.SMEM)]
        + [pl.BlockSpec(memory_space=pltpu.HBM)] * 6,
        out_specs=[pl.BlockSpec(memory_space=pltpu.VMEM)] * peers,
        scratch_shapes=[pltpu.VMEM(x.shape, x.dtype) for x in small]
        + [
            pltpu.VMEM((chunks, volume.shape[0], columns // chunks), volume.dtype),
            pltpu.VMEM((angles, columns), jnp.float32),
            pltpu.VMEM((peers,) + block, jnp.bfloat16),
            pltpu.SemaphoreType.DMA((len(small) + chunks,)),
        ],
        name="project",
    )(place, *small, volume)


def collect_kernel(place, *refs):
    terms, (out, held) = refs[:-2], refs[-2:]
    quarters = 4
    half = place[0] // quarters
    col = place[0] % quarters
    rows, columns = terms[0].shape
    strips = out.shape[1] // 2
    width = out.shape[2]
    low = high = None
    for ref, d in zip(terms, STEPS):
        same = (col - d >= 0) & (col - d < quarters)
        first = jnp.where(same, half, 1 - half) == 0
        weight = jnp.where(first, 1.0, 0.0)
        value = ref[...].astype(jnp.float32)
        low = value * weight if low is None else low + value * weight
        high = value * (1.0 - weight) if high is None else high + value * (1.0 - weight)
    count = 2 * rows * strips
    tile = held.shape[1]
    for h, total in enumerate((low, high)):
        for p in range(strips):
            for t in range(width // tile):
                at = p * width + t * tile
                held[pl.ds(t * count + h * strips + p, rows, stride=2 * strips), :] = total[
                    :, at : at + tile
                ]
    for t in range(width // tile):
        block = held[t * count : (t + 1) * count].astype(jnp.bfloat16)
        out[:, :, t * tile : (t + 1) * tile] = block.reshape(rows, 2 * strips, tile)


def collect(place, terms):
    rows, columns = terms[0].shape
    strips = 4
    shape = (rows, 2 * strips, columns // strips)
    return pl.pallas_call(
        collect_kernel,
        out_shape=jax.ShapeDtypeStruct(shape, jnp.bfloat16),
        in_specs=[pl.BlockSpec(memory_space=pltpu.SMEM)]
        + [pl.BlockSpec(memory_space=pltpu.VMEM)] * len(terms),
        scratch_shapes=[pltpu.VMEM((2 * rows * columns // 128, 128), jnp.float32)],
        compiler_params=pltpu.CompilerParams(vmem_limit_bytes=8 * 2**20),
        name="collect",
    )(place, *terms)


def correlate_kernel(norm, starts, parts, across, owned, out, mixed, sorted_rows, wide):
    blocks, per_block, width = parts.shape
    strips = per_block // 2
    slices, columns = owned.shape
    tile = 128
    tiles = columns // tile
    count = blocks * per_block
    for t in range(width // tile):
        block = parts[:, :, t * tile : (t + 1) * tile].astype(jnp.float32)
        mixed[t * count : (t + 1) * count] = block.reshape(count, tile)
    for core in range(2):
        for high in range(2):
            for p in range(strips):
                for t in range(width // tile):
                    at = (p * width // tile + t) * slices
                    sorted_rows[pl.ds(at + high * 2 + core, blocks // 2, stride=4), :] = mixed[
                        pl.ds(
                            t * count + (core * 2 + high) * strips + p,
                            blocks // 2,
                            stride=2 * per_block,
                        ),
                        :,
                    ]
    rhs = sorted_rows[...].astype(jnp.bfloat16)
    for t in range(tiles):
        owned[:, t * tile : (t + 1) * tile] = rhs[t * slices : (t + 1) * slices]
    wide[...] = across[...].astype(jnp.float32)
    start_slice = starts[0]
    first = starts[1] + LAG
    pieces = []
    for a in range(WZ):
        turn = lax.rem(2 * slices - start_slice - a, slices)
        row = []
        for t in range(tiles):
            block = wide[pl.ds(first + t * tile, ROWS), :]
            row.append(pltpu.roll(block, turn, 1).astype(jnp.bfloat16))
        pieces.append(jnp.concatenate(row, axis=1))
    lhs = jnp.concatenate(pieces, axis=0)
    sums = jnp.dot(lhs, rhs, preferred_element_type=jnp.float32)
    lanes = lax.broadcasted_iota(jnp.int32, (8, tile), 1)
    subs = lax.broadcasted_iota(jnp.int32, (8, tile), 0)
    results = []
    for a in range(WZ):
        total = jnp.zeros((8, tile), jnp.float32)
        for i in range(ROWS // 8):
            block = sums[a * ROWS + i * 8 : a * ROWS + i * 8 + 8]
            if i < WU // 8:
                block = jnp.where(lanes < tile // 2, block, 0.0)
            if i >= tile // 8:
                block = jnp.where(lanes >= tile // 2, block, 0.0)
            total = total + pltpu.roll(block, (-8 * i) % tile, 1)
        aligned = jnp.zeros((8, tile), jnp.float32)
        for d in range(WU):
            here = ((subs - d) & (tile - 1)) == lanes
            value = jnp.sum(jnp.where(here, total, 0.0))
            aligned = jnp.where(lanes == d, value, aligned)
        results.append(aligned[0:1])
    results.append(jnp.zeros((8 - WZ, tile), jnp.float32))
    out[...] = jnp.concatenate(results, axis=0) * norm


def correlate(norm, starts, parts, across):
    blocks, per_block, width = parts.shape
    strips = per_block // 2
    slices, columns = blocks * 2, strips * width
    vmem = pl.BlockSpec(memory_space=pltpu.VMEM)
    return pl.pallas_call(
        functools.partial(correlate_kernel, norm),
        out_shape=[
            jax.ShapeDtypeStruct((slices, columns), jnp.bfloat16),
            jax.ShapeDtypeStruct((8, 128), jnp.float32),
        ],
        in_specs=[pl.BlockSpec(memory_space=pltpu.SMEM), vmem, vmem],
        scratch_shapes=[
            pltpu.VMEM((slices * columns // 128, 128), jnp.float32),
            pltpu.VMEM((slices * columns // 128, 128), jnp.float32),
            pltpu.VMEM(across.shape, jnp.float32),
        ],
        compiler_params=pltpu.CompilerParams(vmem_limit_bytes=14 * 2**20),
        name="correlate",
    )(starts, parts, across)


def finish_kernel(starts, totals, correlation, shifts):
    values = totals[0:WZ, 0:WU]
    correlation[0] = values
    weights = values * values
    lag_slice = starts[0] + lax.broadcasted_iota(jnp.int32, (WZ, WU), 0)
    lag_col = starts[1] + lax.broadcasted_iota(jnp.int32, (WZ, WU), 1)
    count = WZ * WU

    def mean(x):
        return jnp.sum(jnp.sum(x, axis=1, keepdims=True), axis=0, keepdims=True) / count

    denominator = mean(weights) + 1e-06
    by_slice = mean(weights * (lag_slice.astype(jnp.float32) / LAGZ)) / denominator
    by_col = mean(weights * (lag_col.astype(jnp.float32) / LAG)) / denominator
    shifts[...] = jnp.concatenate([by_slice, by_col], axis=1)


def finish(starts, totals):
    return pl.pallas_call(
        finish_kernel,
        out_shape=[
            jax.ShapeDtypeStruct((1, WZ, WU), jnp.float32),
            jax.ShapeDtypeStruct((1, 2), jnp.float32),
        ],
        in_specs=[
            pl.BlockSpec(memory_space=pltpu.SMEM),
            pl.BlockSpec(memory_space=pltpu.VMEM),
        ],
        compiler_params=pltpu.CompilerParams(vmem_limit_bytes=2 * 2**20),
        name="finish",
    )(starts, totals)


def local(
    volume,
    detector_row_weight,
    tile_bank,
    tile_class,
    tile_shift,
    owner_angle,
    measured,
    window_slice,
    window_col,
):
    count = lax.axis_size("zl")
    halves = lax.axis_size("zh")
    peers = count * halves
    line = ("zh", "zl")
    place = lax.axis_index(line).astype(jnp.int32)[None]

    def hop(value, d, keep=None):
        pairs = [(i, (i + d) % peers) for i in range(peers) if keep is None or i % count in keep]
        return lax.ppermute(value, line, pairs)

    items = project(
        place, owner_angle, tile_shift, tile_class, detector_row_weight, tile_bank, volume[0],
        count, halves,
    )
    ahead = hop(items[4], 1, (0, 1))
    behind = hop(items[4], peers - 1, (2, 3))
    got = {d: hop(items[d % peers], d % peers) for d in (2, -2, 1, -1)}
    got[3] = hop(items[3] + ahead, 3)
    got[-3] = hop(items[5] + behind, 5)
    got[0] = items[0]
    packed = collect(place, [got[d] for d in STEPS])
    parts = lax.all_to_all(packed, ("y", "x", "co"), 0, 0, tiled=True)
    seen, _ = lax.optimization_barrier((measured[0], packed))
    slices, quarter = seen.shape
    ring = [(i, (i + 1) % count) for i in range(count)]
    back = [(target, source) for source, target in ring]
    low = lax.ppermute(seen[:, quarter - LAG :], "zl", ring)
    high = lax.ppermute(seen[:, :LAG], "zl", back)
    rest = jnp.zeros((128 - 2 * LAG, slices), jnp.bfloat16)
    across = jnp.concatenate([low.T, seen.T, high.T, rest], axis=0)
    starts = jnp.concatenate([window_slice, window_col])
    norm_factor = 1.0 / math.sqrt(slices * quarter * count)
    owned, part = correlate(norm_factor, starts, parts, across)
    totals, shifts = finish(starts, lax.psum(part, "zl"))
    return (owned[None], totals, shifts.T)


def solution(mesh):
    slab, col = mesh.axis_names
    cols = mesh.shape[col]
    rows = mesh.shape[slab]
    parts = jax.sharding.Mesh(
        mesh.devices.reshape(rows // 16, 4, 2, 2, cols), ("y", "x", "zh", "co", "zl")
    )
    slab = ("y", "x", "zh", "co")
    return jax.shard_map(
        local,
        mesh=parts,
        in_specs=(
            P(slab, "zl", None),
            P(None, "zl"),
            P(),
            P(),
            P(),
            P(),
            P(slab, None, "zl"),
            P(slab),
            P(slab),
        ),
        out_specs=(P(slab, None, "zl"), P(slab, None, None), P(None, slab)),
        check_vma=False,
    )
```

time: 103 us -> 98.1 us (0.952)
  the two profiles are of different devices: /device:TPU:8 before, /device:TPU:16 now
where the time goes in v3:
time: 98.1 us; the launch traced here: 97.6 us
  starting transfers between devices  50.7 us (52%)
  waiting for transfers between devices  20.6 us (21%)
  Pallas kernels  13.1 us (13%)
  blocking collectives  8.34 us (9%)
  other arithmetic  2.31 us (2%)
  between operations  2.14 us (2%)
    ppermute x8, starting transfers between devices, hop(): return lax.ppermute(value, line, pairs)  32.6 us
    ppermute x8, waiting for transfers between devices, hop(): return lax.ppermute(value, line, pairs)  13.6 us
    all_to_all x1, starting transfers between devices, local(): parts = lax.all_to_all(packed, ('y', 'x', 'co'), 0, 0, tiled=True)  10.5 us
    psum x1, blocking collectives, local(): totals, shifts = finish(starts, lax.psum(part, 'zl'))  8.34 us
    pallas_call x1, Pallas kernels, project(): pl.pallas_call(project_kernel, out_shape=[jax.ShapeDtypeStruct(block, jnp...  8.28 us
    all_to_all x1, waiting for transfers between devices, local(): parts = lax.all_to_all(packed, ('y', 'x', 'co'), 0, 0, tiled=True)  5.77 us
    ppermute x1, starting transfers between devices, local(): high = lax.ppermute(seen[:, :LAG], 'zl', back)  5.72 us
    pallas_call x1, Pallas kernels, correlate(): pl.pallas_call(functools.partial(correlate_kernel, norm), out_shape=[jax....  1.99 us
  transfers between devices with their start and end apart: 11, of which 4 were waited for; matrix products, arithmetic and copies ran while one was open for 3% of the time, Pallas kernels for 0%

profile of v3, /device:TPU:16, one launch (start us, length us, event | category | flops | bytes accessed | tf_op | source)
XLA Modules:
  0.0 97.6 jit_solution(12629340193280514816)
XLA Ops:
  0.6 8.3 %project.1 = (bf16[64,1536]{1,0:T(8,128)(2,1)}, bf16[64,1536]{1,0:T(8,128)(2,1)}, bf16[64,1536]{1,0:T(8,128)(2,1)}, bf16[64,1536]{1,0:T(8,128)(2,1)}, bf16[64,15...) custom-call(s32[1]{0:T(128)} %bitcast.place, ...), custom_call_target="tpu_custom_call" | custom-call | tf_op jit(solution)/shard_map/project/pallas_call | solution.py:100
  9.0 0.8 collective-permute-start.6
  9.8 4.9 %collective-permute-start.4 = (bf16[64,1536]{1,0:T(8,128)(2,1)}, bf16[64,1536]{1,0:T(8,128)(2,1)S(1)}, u32[]{:S(2)}, u32[]{:S(2)}) collective-permute-start(bf16[64,1536]{1,0:T(8,128)(2,1)} %get-tuple-element.22), channel_id=1, source_target_pairs={{0,1},{1,2},{8,9},{9,10},{4,5},{5,6},{12,13},{13,14},{16,17},{17,1... | collective-permute-start | bytes 589832 | tf_op jit(solution)/shard_map/ppermute | solution.py:297
  14.7 4.9 %collective-permute-start = (bf16[64,1536]{1,0:T(8,128)(2,1)}, bf16[64,1536]{1,0:T(8,128)(2,1)S(1)}, u32[]{:S(2)}, u32[]{:S(2)}) collective-permute-start(bf16[64,1536]{1,0:T(8,128)(2,1)} %get-tuple-element.17), channel_id=1, source_target_pairs={{0,1},{1,2},{2,3},{3,8},{8,9},{9,10},{10,11},{11,0},{4,5},{5,6},{6... | collective-permute-start | bytes 589832 | tf_op jit(solution)/shard_map/ppermute | solution.py:297
  19.6 5.5 %collective-permute-start.1 = (bf16[64,1536]{1,0:T(8,128)(2,1)}, bf16[64,1536]{1,0:T(8,128)(2,1)S(1)}, u32[]{:S(2)}, u32[]{:S(2)}) collective-permute-start(bf16[64,1536]{1,0:T(8,128)(2,1)} %get-tuple-element.18), channel_id=1, source_target_pairs={{0,11},{1,0},{2,1},{3,2},{8,3},{9,8},{10,9},{11,10},{4,15},{5,4},{... | collective-permute-start | bytes 589832 | tf_op jit(solution)/shard_map/ppermute | solution.py:297
  25.1 1.9 %collective-permute-start.2 = (bf16[64,1536]{1,0:T(8,128)(2,1)}, bf16[64,1536]{1,0:T(8,128)(2,1)S(1)}, u32[]{:S(2)}, u32[]{:S(2)}) collective-permute-start(bf16[64,1536]{1,0:T(8,128)(2,1)} %get-tuple-element.19), channel_id=1, source_target_pairs={{0,2},{1,3},{2,8},{3,9},{8,10},{9,11},{10,0},{11,1},{4,6},{5,7},{6... | collective-permute-start | bytes 589832 | tf_op jit(solution)/shard_map/ppermute | solution.py:297
  27.1 6.0 %collective-permute-start.3 = (bf16[64,1536]{1,0:T(8,128)(2,1)}, bf16[64,1536]{1,0:T(8,128)(2,1)S(1)}, u32[]{:S(2)}, u32[]{:S(2)}) collective-permute-start(bf16[64,1536]{1,0:T(8,128)(2,1)} %get-tuple-element.20), channel_id=1, source_target_pairs={{0,10},{1,11},{2,0},{3,1},{8,2},{9,3},{10,8},{11,9},{4,14},{5,15},... | collective-permute-start | bytes 589832 | tf_op jit(solution)/shard_map/ppermute | solution.py:297
  33.1 1.0 %add.13 = bf16[64,1536]{1,0:T(8,128)(2,1)S(1)} add(bf16[64,1536]{1,0:T(8,128)(2,1)} %get-tuple-element.23, bf16[64,1536]{1,0:T(8,128)(2,1)S(1)} %collective-permute-done.6) | non-fusion elementwise | flops 98304 | bytes 589824 | tf_op jit(solution)/shard_map/add | solution.py:307
  34.1 6.6 %collective-permute-start.7 = (bf16[64,1536]{1,0:T(8,128)(2,1)S(1)}, bf16[64,1536]{1,0:T(8,128)(2,1)S(1)}, u32[]{:S(2)}, u32[]{:S(2)}) collective-permute-start(bf16[64,1536]{1,0:T(8,128)(2,1)S(1)} %add.13), channel_id=1, source_target_pairs={{0,9},{1,10},{2,11},{3,0},{8,1},{9,2},{10,3},{11,8},{4,13},{5,14},... | collective-permute-start | bytes 589832 | tf_op jit(solution)/shard_map/ppermute | solution.py:297
  40.7 1.0 %add.12 = bf16[64,1536]{1,0:T(8,128)(2,1)S(1)} add(bf16[64,1536]{1,0:T(8,128)(2,1)} %get-tuple-element.21, bf16[64,1536]{1,0:T(8,128)(2,1)S(1)} %collective-permute-done.4) | non-fusion elementwise | flops 98304 | bytes 589824 | tf_op jit(solution)/shard_map/add | solution.py:306
  41.7 1.9 %collective-permute-start.5 = (bf16[64,1536]{1,0:T(8,128)(2,1)S(1)}, bf16[64,1536]{1,0:T(8,128)(2,1)S(1)}, u32[]{:S(2)}, u32[]{:S(2)}) collective-permute-start(bf16[64,1536]{1,0:T(8,128)(2,1)S(1)} %add.12), channel_id=1, source_target_pairs={{0,3},{1,8},{2,9},{3,10},{8,11},{9,0},{10,1},{11,2},{4,7},{5,12},{... | collective-permute-start | bytes 589832 | tf_op jit(solution)/shard_map/ppermute | solution.py:297
  43.6 0.2 copy.12
  45.2 4.3 %collective-permute-done.7.refs_6_ = bf16[64,1536]{1,0:T(8,128)(2,1)S(1)} collective-permute-done((bf16[64,1536]{1,0:T(8,128)(2,1)S(1)}, bf16[64,1536]{1,0:T(8,128)(2,1)S(1)}, u32[]{:S(2)}, u32[]{:S(2)}) %collective-permute-start.7) | collective-permute-done | bytes 196640 | tf_op jit(solution)/shard_map/ppermute | solution.py:297
  49.5 9.3 %collective-permute-done.5.refs_5_ = bf16[64,1536]{1,0:T(8,128)(2,1)S(1)} collective-permute-done((bf16[64,1536]{1,0:T(8,128)(2,1)S(1)}, bf16[64,1536]{1,0:T(8,128)(2,1)S(1)}, u32[]{:S(2)}, u32[]{:S(2)}) %collective-permute-start.5) | collective-permute-done | bytes 196640 | tf_op jit(solution)/shard_map/ppermute | solution.py:297
  58.8 1.7 %collect.1 = bf16[64,8,384]{2,1,0:T(8,128)(2,1)} custom-call(s32[1]{0:T(128)} %bitcast.place, bf16[64,1536]{1,0:T(8,128)(2,1)S(1)} %copy-done, bf16[64,1536]{1,0:T(8,128)(2,1)S(1)} %collective-permute-done.refs_1_, bf16[64,1536]{1,0:T(8,128)(2,1)S(1)} %collective-permute-done.1.refs_2_, bf16[64,1536]{1,0:T(8,128)(2,1)S(1)} %collective-permute-done.2.refs_3_, ...), custom_call_target="tpu_custom_call" | custom-call | tf_op jit(solution)/shard_map/collect/pallas_call | solution.py:151
  60.5 10.5 %all-to-all-start = ((bf16[64,8,384]{2,1,0:T(8,128)(2,1)}), bf16[64,8,384]{2,1,0:T(8,128)(2,1)S(1)}, u32[]{:S(2)}, u32[]{:S(2)}) async-start(bf16[64,8,384]{2,1,0:T(8,128)(2,1)} %collect.1), calls=%async_computation | async-start | bytes 786432 | tf_op jit(solution)/shard_map/all_to_all | solution.py:310
  71.0 1.9 %collective-permute-start.8 = (bf16[128,32]{0,1:T(8,128)(2,1)S(1)}, bf16[128,32]{0,1:T(8,128)(2,1)S(1)}, u32[]{:S(2)}, u32[]{:S(2)}) collective-permute-start(bf16[128,32]{0,1:T(8,128)(2,1)S(1)} %get-tuple-element.29), channel_id=1, source_target_pairs={{0,1},{1,2},{2,3},{3,0},{4,5},{5,6},{6,7},{7,4},{8,9},{9,10},{10,1... | collective-permute-start | bytes 24584 | tf_op jit(solution)/shard_map/ppermute | solution.py:315
  72.9 5.7 %collective-permute-start.9 = (bf16[128,32]{0,1:T(8,128)(2,1)S(1)}, bf16[128,32]{0,1:T(8,128)(2,1)S(1)}, u32[]{:S(2)}, u32[]{:S(2)}) collective-permute-start(bf16[128,32]{0,1:T(8,128)(2,1)S(1)} %get-tuple-element.30), channel_id=1, source_target_pairs={{1,0},{2,1},{3,2},{0,3},{5,4},{6,5},{7,6},{4,7},{9,8},{10,9},{11,1... | collective-permute-start | bytes 24584 | tf_op jit(solution)/shard_map/ppermute | solution.py:316
  78.8 1.2 %collective-permute-done.9 = bf16[128,32]{0,1:T(8,128)(2,1)S(1)} collective-permute-done((bf16[128,32]{0,1:T(8,128)(2,1)S(1)}, bf16[128,32]{0,1:T(8,128)(2,1)S(1)}, u32[]{:S(2)}, u32[]{:S(2)}) %collective-permute-start.9) | collective-permute-done | bytes 8224 | tf_op jit(solution)/shard_map/ppermute | solution.py:316
  80.0 0.3 maximum_maximum_fusion.across
  80.3 5.8 %all-to-all-done.parts = bf16[64,8,384]{2,1,0:T(8,128)(2,1)S(1)} async-done(((bf16[64,8,384]{2,1,0:T(8,128)(2,1)}), bf16[64,8,384]{2,1,0:T(8,128)(2,1)S(1)}, u32[]{:S(2)}, u32[]{:S(2)}) %all-to-all-start) | async-done | bytes 393248 | tf_op jit(solution)/shard_map/all_to_all | solution.py:310
  86.1 2.0 %correlate.1 = (bf16[128,1536]{1,0:T(8,128)(2,1)}, f32[8,128]{1,0:T(8,128)S(1)}) custom-call(s32[2]{0:T(128)S(1)} %pad_add_fusion.starts, bf16[64,8,384]{2,1,0:T(8,128)(2,1)S(1)} %all-to-all-done.parts, bf16[1664,128]{1,0:T(8,128)(2,1)S(1)} %maximum_maximum_fusion.across), custom_call_target="tpu_custom_call" | custom-call | tf_op jit(solution)/shard_map/correlate/pallas_call | solution.py:228
  88.1 8.3 %psum.7.totals = f32[8,128]{1,0:T(8,128)S(1)} all-reduce(f32[8,128]{1,0:T(8,128)S(1)} %get-tuple-element.26), channel_id=1, replica_groups=mesh['y'=8,'x'=4,'zh'=2,'co'=2,'zl'=4] {'zl'}, use_global_device_ids=true, to_apply=%region_0.0 | all-reduce | flops 1024 | bytes 8192 | tf_op jit(solution)/shard_map/psum | solution.py:322
  96.4 1.1 %finish.1 = (f32[1,4,16]{2,1,0:T(4,128)}, f32[1,2]{1,0:T(1,128)}) custom-call(s32[2]{0:T(128)S(1)} %pad_add_fusion.starts, f32[8,128]{1,0:T(8,128)S(1)} %psum.7.totals), custom_call_target="tpu_custom_call" | custom-call | tf_op jit(solution)/shard_map/finish/pallas_call | solution.py:263
  (15 shorter events, 0.2 us)
Async XLA Ops:
  0.6 43.0 %copy-start.1 = (bf16[1,128,1536]{2,1,0:T(8,128)(2,1)S(1)}, bf16[1,128,1536]{2,1,0:T(8,128)(2,1)}, u32[]{:S(2)}) copy-start(bf16[1,128,1536]{2,1,0:T(8,128)(2,1)} %param.15) | copy-start | bytes 1179652
  8.9 49.9 %copy-start = (bf16[64,1536]{1,0:T(8,128)(2,1)S(1)}, bf16[64,1536]{1,0:T(8,128)(2,1)}, u32[]{:S(2)}) copy-start(bf16[64,1536]{1,0:T(8,128)(2,1)} %get-tuple-element.16.refs_0_) | copy-start | bytes 589828
  9.0 18.1 %collective-permute-start.6 = (bf16[64,1536]{1,0:T(8,128)(2,1)}, bf16[64,1536]{1,0:T(8,128)(2,1)S(1)}, u32[]{:S(2)}, u32[]{:S(2)}) collective-permute-start(bf16[64,1536]{1,0:T(8,128)(2,1)} %get-tuple-element.22), channel_id=1, source_target_pairs={{2,1},{3,2},{10,9},{11,10},{6,5},{7,6},{14,13},{15,14},{18,17},{19... | collective-permute-start | bytes 589832 | tf_op jit(solution)/shard_map/ppermute | solution.py:297
  9.8 24.3 %collective-permute-start.4 = (bf16[64,1536]{1,0:T(8,128)(2,1)}, bf16[64,1536]{1,0:T(8,128)(2,1)S(1)}, u32[]{:S(2)}, u32[]{:S(2)}) collective-permute-start(bf16[64,1536]{1,0:T(8,128)(2,1)} %get-tuple-element.22), channel_id=1, source_target_pairs={{0,1},{1,2},{8,9},{9,10},{4,5},{5,6},{12,13},{13,14},{16,17},{17,1... | collective-permute-start | bytes 589832 | tf_op jit(solution)/shard_map/ppermute | solution.py:297
  14.7 27.0 %collective-permute-start = (bf16[64,1536]{1,0:T(8,128)(2,1)}, bf16[64,1536]{1,0:T(8,128)(2,1)S(1)}, u32[]{:S(2)}, u32[]{:S(2)}) collective-permute-start(bf16[64,1536]{1,0:T(8,128)(2,1)} %get-tuple-element.17), channel_id=1, source_target_pairs={{0,1},{1,2},{2,3},{3,8},{8,9},{9,10},{10,11},{11,0},{4,5},{5,6},{6... | collective-permute-start | bytes 589832 | tf_op jit(solution)/shard_map/ppermute | solution.py:297
  19.6 25.6 %collective-permute-start.1 = (bf16[64,1536]{1,0:T(8,128)(2,1)}, bf16[64,1536]{1,0:T(8,128)(2,1)S(1)}, u32[]{:S(2)}, u32[]{:S(2)}) collective-permute-start(bf16[64,1536]{1,0:T(8,128)(2,1)} %get-tuple-element.18), channel_id=1, source_target_pairs={{0,11},{1,0},{2,1},{3,2},{8,3},{9,8},{10,9},{11,10},{4,15},{5,4},{... | collective-permute-start | bytes 589832 | tf_op jit(solution)/shard_map/ppermute | solution.py:297
  25.1 20.0 %collective-permute-start.2 = (bf16[64,1536]{1,0:T(8,128)(2,1)}, bf16[64,1536]{1,0:T(8,128)(2,1)S(1)}, u32[]{:S(2)}, u32[]{:S(2)}) collective-permute-start(bf16[64,1536]{1,0:T(8,128)(2,1)} %get-tuple-element.19), channel_id=1, source_target_pairs={{0,2},{1,3},{2,8},{3,9},{8,10},{9,11},{10,0},{11,1},{4,6},{5,7},{6... | collective-permute-start | bytes 589832 | tf_op jit(solution)/shard_map/ppermute | solution.py:297
  27.1 18.1 %collective-permute-start.3 = (bf16[64,1536]{1,0:T(8,128)(2,1)}, bf16[64,1536]{1,0:T(8,128)(2,1)S(1)}, u32[]{:S(2)}, u32[]{:S(2)}) collective-permute-start(bf16[64,1536]{1,0:T(8,128)(2,1)} %get-tuple-element.20), channel_id=1, source_target_pairs={{0,10},{1,11},{2,0},{3,1},{8,2},{9,3},{10,8},{11,9},{4,14},{5,15},... | collective-permute-start | bytes 589832 | tf_op jit(solution)/shard_map/ppermute | solution.py:297
  34.1 15.4 %collective-permute-start.7 = (bf16[64,1536]{1,0:T(8,128)(2,1)S(1)}, bf16[64,1536]{1,0:T(8,128)(2,1)S(1)}, u32[]{:S(2)}, u32[]{:S(2)}) collective-permute-start(bf16[64,1536]{1,0:T(8,128)(2,1)S(1)} %add.13), channel_id=1, source_target_pairs={{0,9},{1,10},{2,11},{3,0},{8,1},{9,2},{10,3},{11,8},{4,13},{5,14},... | collective-permute-start | bytes 589832 | tf_op jit(solution)/shard_map/ppermute | solution.py:297
  41.7 17.1 %collective-permute-start.5 = (bf16[64,1536]{1,0:T(8,128)(2,1)S(1)}, bf16[64,1536]{1,0:T(8,128)(2,1)S(1)}, u32[]{:S(2)}, u32[]{:S(2)}) collective-permute-start(bf16[64,1536]{1,0:T(8,128)(2,1)S(1)} %add.12), channel_id=1, source_target_pairs={{0,3},{1,8},{2,9},{3,10},{8,11},{9,0},{10,1},{11,2},{4,7},{5,12},{... | collective-permute-start | bytes 589832 | tf_op jit(solution)/shard_map/ppermute | solution.py:297
  60.5 25.5 %all-to-all-start = ((bf16[64,8,384]{2,1,0:T(8,128)(2,1)}), bf16[64,8,384]{2,1,0:T(8,128)(2,1)S(1)}, u32[]{:S(2)}, u32[]{:S(2)}) async-start(bf16[64,8,384]{2,1,0:T(8,128)(2,1)} %collect.1), calls=%async_computation | async-start | bytes 786432 | tf_op jit(solution)/shard_map/all_to_all | solution.py:310
  71.0 7.8 %collective-permute-start.8 = (bf16[128,32]{0,1:T(8,128)(2,1)S(1)}, bf16[128,32]{0,1:T(8,128)(2,1)S(1)}, u32[]{:S(2)}, u32[]{:S(2)}) collective-permute-start(bf16[128,32]{0,1:T(8,128)(2,1)S(1)} %get-tuple-element.29), channel_id=1, source_target_pairs={{0,1},{1,2},{2,3},{3,0},{4,5},{5,6},{6,7},{7,4},{8,9},{9,10},{10,1... | collective-permute-start | bytes 24584 | tf_op jit(solution)/shard_map/ppermute | solution.py:315
  72.9 7.1 %collective-permute-start.9 = (bf16[128,32]{0,1:T(8,128)(2,1)S(1)}, bf16[128,32]{0,1:T(8,128)(2,1)S(1)}, u32[]{:S(2)}, u32[]{:S(2)}) collective-permute-start(bf16[128,32]{0,1:T(8,128)(2,1)S(1)} %get-tuple-element.30), channel_id=1, source_target_pairs={{1,0},{2,1},{3,2},{0,3},{5,4},{6,5},{7,6},{4,7},{9,8},{10,9},{11,1... | collective-permute-start | bytes 24584 | tf_op jit(solution)/shard_map/ppermute | solution.py:316

commit v4 on v2

v4 whole, which is shorter than its diff:
```python
import functools
import math

import jax
import jax.numpy as jnp
from jax import lax
from jax.experimental import pallas as pl
from jax.experimental.pallas import tpu as pltpu
from jax.sharding import PartitionSpec as P

LAG = 32
WU = 16
LAGZ = 4
WZ = 4
ROWS = 144


def project_kernel(*refs):
    sources, out, rest = refs[:6], refs[6], refs[7:]
    owner, shift, cls, weights, bank, volume, spreadable, held, mixed, ready, sems = rest
    angles = weights.shape[0]
    columns = volume.shape[1]
    tile = bank.shape[1]
    banks = bank.shape[0]
    tiles = columns // tile
    peers, strips, width = ready.shape
    quarters = peers // angles
    per = tiles // quarters
    coarse = 8
    ring = tiles // coarse
    pair = 2 * tile
    small = [
        pltpu.make_async_copy(source, target, sems.at[i])
        for i, (source, target) in enumerate(zip(sources[:5], rest[:5]))
    ]
    large = []
    for r in range(coarse // 2):
        for j in range(ring):
            where = pl.ds(j * coarse * tile + r * pair, pair)
            large.append(
                pltpu.make_async_copy(
                    sources[5].at[:, where], volume.at[:, where], sems.at[5 + len(large)]
                )
            )
    for copy in small + large:
        copy.start()
    for copy in small:
        copy.wait()
    lane = lax.broadcasted_iota(jnp.int32, (angles, angles), 1)
    wide = jnp.broadcast_to(owner[...].astype(jnp.float32), (angles, angles))
    onehot = (wide.T.astype(jnp.int32) == lane).astype(jnp.float32)
    shifts = jnp.sum(onehot * shift[...].astype(jnp.float32), axis=1, keepdims=True)
    classes = jnp.sum(onehot * cls[...].astype(jnp.float32), axis=1, keepdims=True)
    shifts = jnp.broadcast_to(shifts.astype(jnp.int32), (angles, tile))
    chosen = jnp.dot(
        onehot.astype(jnp.bfloat16), weights[...], preferred_element_type=jnp.float32
    ).astype(jnp.bfloat16)
    classes = jnp.broadcast_to(classes, (angles, tile)).astype(jnp.int32)
    masks = [(classes == c).astype(jnp.bfloat16) for c in range(banks)]
    stacked = bank[...].reshape(banks * tile, tile)
    group = 8
    for r in range(coarse // 2):
        for j in range(ring):
            large[r * ring + j].wait()
            at = j * coarse * tile + r * pair
            ray = jnp.dot(
                chosen, volume[:, at : at + pair], preferred_element_type=jnp.float32
            ).astype(jnp.bfloat16)
            for s in range(2):
                piece = ray[:, s * tile : (s + 1) * tile]
                for c in range(banks):
                    spreadable[
                        s, j * angles : (j + 1) * angles, c * tile : (c + 1) * tile
                    ] = piece * masks[c]
        for s in range(2):
            spread = jnp.dot(spreadable[s], stacked, preferred_element_type=jnp.float32)
            for g in range(angles // group):
                rows = slice(g * group, (g + 1) * group)
                parts = [
                    spread[j * angles + g * group : j * angles + (g + 1) * group]
                    for j in range(ring)
                ]
                for b in range(3):
                    keep = ((shifts[rows] >> (3 + b)) & 1) == 0
                    parts = [
                        jnp.where(keep, parts[j], parts[(j - (1 << b)) % ring])
                        for j in range(ring)
                    ]
                for j in range(ring):
                    at = (j * coarse + 2 * r + s) * tile
                    held[rows, at : at + tile] = parts[j]
    inner = width // tile
    count = angles * strips
    copies = []
    for q in range(quarters):
        for g in range(angles // group):
            rows = slice(g * group, (g + 1) * group)
            parts = []
            for t in range(q * per - coarse + 1, (q + 1) * per):
                at = t % tiles * tile
                parts.append(held[rows, at : at + tile])
            for b in (2, 1, 0):
                step = 1 << b
                keep = ((shifts[rows] >> b) & 1) == 0
                parts = [
                    jnp.where(keep, parts[i], parts[i - step]) for i in range(step, len(parts))
                ]
            for c in range(per):
                p, t = divmod(c, inner)
                at = (q * inner + t) * count + g * group * strips + p
                mixed[pl.ds(at, group, stride=strips), :] = parts[c]
        where = slice(q * angles, (q + 1) * angles)
        for t in range(inner):
            at = (q * inner + t) * count
            block = mixed[at : at + count].astype(jnp.bfloat16)
            ready[where, :, t * tile : (t + 1) * tile] = block.reshape(angles, strips, tile)
        copies.append(pltpu.make_async_copy(ready.at[where], out.at[where], sems.at[q]))
        copies[-1].start()
    for copy in copies:
        copy.wait()


def project(owner, shift, cls, weights, bank, volume, quarters):
    angles = weights.shape[0]
    columns = volume.shape[1]
    tile = bank.shape[1]
    shape = (quarters * angles, 4, columns // quarters // 4)
    small = (owner[None], shift[None], cls[None], weights, bank)
    hbm = pl.BlockSpec(memory_space=pltpu.HBM)
    return pl.pallas_call(
        project_kernel,
        out_shape=jax.ShapeDtypeStruct(shape, jnp.bfloat16),
        in_specs=[hbm] * 6,
        out_specs=hbm,
        scratch_shapes=[pltpu.VMEM(x.shape, x.dtype) for x in small + (volume,)]
        + [
            pltpu.VMEM((2, columns // tile // 8 * angles, bank.shape[0] * tile), jnp.bfloat16),
            pltpu.VMEM((angles, columns), jnp.float32),
            pltpu.VMEM((angles * columns // tile, tile), jnp.float32),
            pltpu.VMEM(shape, jnp.bfloat16),
            pltpu.SemaphoreType.DMA((len(small) + columns // tile // 2,)),
        ],
        name="project",
    )(*small, volume)


def correlate_kernel(norm, starts, parts, across, owned, out, mixed, wide):
    peers, strips, width = parts.shape
    slices, columns = owned.shape
    tile = 128
    tiles = columns // tile
    inner = width // tile
    count = slices * strips
    group = 16
    for g in range(slices // group):
        total = jnp.zeros((group, strips, width), jnp.float32)
        for c in range(peers // slices):
            at = c * slices + g * group
            total = total + parts[at : at + group].astype(jnp.float32)
        for t in range(inner):
            at = t * count + g * group * strips
            block = total[:, :, t * tile : (t + 1) * tile]
            mixed[at : at + group * strips] = block.reshape(group * strips, tile)
    stack = []
    for p in range(strips):
        for t in range(inner):
            block = mixed[pl.ds(t * count + p, slices, stride=strips), :].astype(jnp.bfloat16)
            at = (p * inner + t) * tile
            owned[:, at : at + tile] = block
            stack.append(block)
    rhs = jnp.concatenate(stack, axis=0)
    wide[...] = across[...].astype(jnp.float32)
    start_slice = starts[0]
    first = starts[1] + LAG
    pieces = []
    for a in range(WZ):
        turn = lax.rem(2 * slices - start_slice - a, slices)
        row = []
        for t in range(tiles):
            block = wide[pl.ds(first + t * tile, ROWS), :]
            row.append(pltpu.roll(block, turn, 1).astype(jnp.bfloat16))
        pieces.append(jnp.concatenate(row, axis=1))
    lhs = jnp.concatenate(pieces, axis=0)
    sums = jnp.dot(lhs, rhs, preferred_element_type=jnp.float32)
    lanes = lax.broadcasted_iota(jnp.int32, (8, tile), 1)
    subs = lax.broadcasted_iota(jnp.int32, (8, tile), 0)
    results = []
    for a in range(WZ):
        total = jnp.zeros((8, tile), jnp.float32)
        for i in range(ROWS // 8):
            block = sums[a * ROWS + i * 8 : a * ROWS + i * 8 + 8]
            if i < WU // 8:
                block = jnp.where(lanes < tile // 2, block, 0.0)
            if i >= tile // 8:
                block = jnp.where(lanes >= tile // 2, block, 0.0)
            total = total + pltpu.roll(block, (-8 * i) % tile, 1)
        aligned = jnp.zeros((8, tile), jnp.float32)
        for d in range(WU):
            here = ((subs - d) & (tile - 1)) == lanes
            value = jnp.sum(jnp.where(here, total, 0.0))
            aligned = jnp.where(lanes == d, value, aligned)
        results.append(aligned[0:1])
    results.append(jnp.zeros((8 - WZ, tile), jnp.float32))
    out[...] = jnp.concatenate(results, axis=0) * norm


def correlate(norm, starts, parts, across):
    peers, strips, width = parts.shape
    slices, columns = across.shape[1], strips * width
    vmem = pl.BlockSpec(memory_space=pltpu.VMEM)
    return pl.pallas_call(
        functools.partial(correlate_kernel, norm),
        out_shape=[
            jax.ShapeDtypeStruct((slices, columns), jnp.bfloat16),
            jax.ShapeDtypeStruct((8, 128), jnp.float32),
        ],
        in_specs=[pl.BlockSpec(memory_space=pltpu.SMEM), vmem, vmem],
        scratch_shapes=[
            pltpu.VMEM((slices * columns // 128, 128), jnp.float32),
            pltpu.VMEM(across.shape, jnp.float32),
        ],
        compiler_params=pltpu.CompilerParams(vmem_limit_bytes=14 * 2**20),
        name="correlate",
    )(starts, parts, across)


def finish_kernel(starts, totals, correlation, shifts):
    values = totals[0:WZ, 0:WU]
    correlation[0] = values
    weights = values * values
    lag_slice = starts[0] + lax.broadcasted_iota(jnp.int32, (WZ, WU), 0)
    lag_col = starts[1] + lax.broadcasted_iota(jnp.int32, (WZ, WU), 1)
    count = WZ * WU

    def mean(x):
        return jnp.sum(jnp.sum(x, axis=1, keepdims=True), axis=0, keepdims=True) / count

    denominator = mean(weights) + 1e-06
    by_slice = mean(weights * (lag_slice.astype(jnp.float32) / LAGZ)) / denominator
    by_col = mean(weights * (lag_col.astype(jnp.float32) / LAG)) / denominator
    shifts[...] = jnp.concatenate([by_slice, by_col], axis=1)


def finish(starts, totals):
    return pl.pallas_call(
        finish_kernel,
        out_shape=[
            jax.ShapeDtypeStruct((1, WZ, WU), jnp.float32),
            jax.ShapeDtypeStruct((1, 2), jnp.float32),
        ],
        in_specs=[
            pl.BlockSpec(memory_space=pltpu.SMEM),
            pl.BlockSpec(memory_space=pltpu.VMEM),
        ],
        compiler_params=pltpu.CompilerParams(vmem_limit_bytes=2 * 2**20),
        name="finish",
    )(starts, totals)


def local(
    volume,
    detector_row_weight,
    tile_bank,
    tile_class,
    tile_shift,
    owner_angle,
    measured,
    window_slice,
    window_col,
):
    count = lax.axis_size("zl")
    pieces = project(
        owner_angle, tile_shift, tile_class, detector_row_weight, tile_bank, volume[0], count
    )
    parts = lax.all_to_all(pieces, ("zl", "y", "x", "zh", "co"), 0, 0, tiled=True)
    seen, _ = lax.optimization_barrier((measured[0], pieces))
    slices, quarter = seen.shape
    ring = [(i, (i + 1) % count) for i in range(count)]
    back = [(target, source) for source, target in ring]
    low = lax.ppermute(seen[:, quarter - LAG :], "zl", ring)
    high = lax.ppermute(seen[:, :LAG], "zl", back)
    rest = jnp.zeros((128 - 2 * LAG, slices), jnp.bfloat16)
    across = jnp.concatenate([low.T, seen.T, high.T, rest], axis=0)
    starts = jnp.concatenate([window_slice, window_col])
    norm_factor = 1.0 / math.sqrt(slices * quarter * count)
    owned, part = correlate(norm_factor, starts, parts, across)
    totals, shifts = finish(starts, lax.psum(part, "zl"))
    return (owned[None], totals, shifts.T)


def solution(mesh):
    slab, col = mesh.axis_names
    cols = mesh.shape[col]
    rows = mesh.shape[slab]
    parts = jax.sharding.Mesh(
        mesh.devices.reshape(rows // 16, 4, 2, 2, cols), ("y", "x", "zh", "co", "zl")
    )
    slab = ("y", "x", "zh", "co")
    return jax.shard_map(
        local,
        mesh=parts,
        in_specs=(
            P(slab, "zl", None),
            P(None, "zl"),
            P(),
            P(),
            P(),
            P(),
            P(slab, None, "zl"),
            P(slab),
            P(slab),
        ),
        out_specs=(P(slab, None, "zl"), P(slab, None, None), P(None, slab)),
        check_vma=False,
    )
```

time: 103 us -> 88.8 us (0.86)
  the two profiles are of different devices: /device:TPU:8 before, /device:TPU:2 now
where the time goes in v4:
time: 88.8 us; the launch traced here: 88.5 us
  waiting for transfers between devices  33 us (37%)
  starting transfers between devices  29.8 us (34%)
  Pallas kernels  13.1 us (15%)
  blocking collectives  10.1 us (11%)
  between operations  2 us (2%)
    all_to_all x1, waiting for transfers between devices, local(): lax.all_to_all(pieces, ('zl', 'y', 'x', 'zh', 'co'), 0, 0, tiled=True)  23.4 us
    all_to_all x1, starting transfers between devices, local(): lax.all_to_all(pieces, ('zl', 'y', 'x', 'zh', 'co'), 0, 0, tiled=True)  21.2 us
    psum x1, blocking collectives, local(): totals, shifts = finish(starts, lax.psum(part, 'zl'))  10.1 us
    pallas_call x1, Pallas kernels, project(): pl.pallas_call(project_kernel, out_shape=jax.ShapeDtypeStruct(shape, jnp....  9.76 us
    ppermute x1, waiting for transfers between devices, local(): high = lax.ppermute(seen[:, :LAG], 'zl', back)  9.56 us
    ppermute x1, starting transfers between devices, local(): high = lax.ppermute(seen[:, :LAG], 'zl', back)  6.65 us
    pallas_call x1, Pallas kernels, correlate(): pl.pallas_call(functools.partial(correlate_kernel, norm), out_shape=[jax....  2.18 us
    ppermute x1, starting transfers between devices, local(): low = lax.ppermute(seen[:, quarter - LAG:], 'zl', ring)  1.92 us
  transfers between devices with their start and end apart: 3, of which 2 were waited for; matrix products, arithmetic and copies ran while one was open for 1% of the time, Pallas kernels for 0%

profile of v4, /device:TPU:2, one launch (start us, length us, event | category | flops | bytes accessed | tf_op | source)
XLA Modules:
  0.0 88.5 jit_solution(6694928205660936383)
XLA Ops:
  0.6 9.8 %project.1 = bf16[512,4,384]{2,1,0:T(4,128)(2,1)} custom-call(s32[1,128]{1,0:T(1,128)} %bitcast.15, s32[1,128]{1,0:T(1,128)} %bitcast.16, s32[1,128]{1,0:T(1,128)} %bitcast.17, bf16[128,128]{1,0:T(8,128)(2,1)} %refs_3_.1, bf16[4,128,128]{2,1,0:T(8,128)(2,1)} %refs_4_.1, bf16[128,6144]{1,0:T(8,128)(2,1)} %bitcast.12), custom_call_target="tpu_custom_call" | custom-call | tf_op jit(solution)/shard_map/project/pallas_call | solution.py:130
  10.4 0.0 copy-start
  10.4 21.2 %all-to-all-start = ((bf16[512,4,384]{2,1,0:T(4,128)(2,1)}), bf16[512,4,384]{2,1,0:T(4,128)(2,1)S(1)}, u32[]{:S(2)}, u32[]{:S(2)}) async-start(bf16[512,4,384]{2,1,0:T(4,128)(2,1)} %project.1), calls=%async_computation | async-start | bytes 3145728 | tf_op jit(solution)/shard_map/all_to_all | solution.py:275
  31.6 0.0 copy-done
  31.6 0.2 copy.12
  31.9 6.7 %collective-permute-start.1 = (bf16[128,32]{0,1:T(8,128)(2,1)S(1)}, bf16[128,32]{0,1:T(8,128)(2,1)S(1)}, u32[]{:S(2)}, u32[]{:S(2)}) collective-permute-start(bf16[128,32]{0,1:T(8,128)(2,1)S(1)} %get-tuple-element.14), channel_id=1, source_target_pairs={{1,0},{2,1},{3,2},{0,3},{5,4},{6,5},{7,6},{4,7},{9,8},{10,9},{11,1... | collective-permute-start | bytes 24584 | tf_op jit(solution)/shard_map/ppermute | solution.py:281
  38.5 1.9 %collective-permute-start = (bf16[128,32]{0,1:T(8,128)(2,1)S(1)}, bf16[128,32]{0,1:T(8,128)(2,1)S(1)}, u32[]{:S(2)}, u32[]{:S(2)}) collective-permute-start(bf16[128,32]{0,1:T(8,128)(2,1)S(1)} %get-tuple-element.13), channel_id=1, source_target_pairs={{0,1},{1,2},{2,3},{3,0},{4,5},{5,6},{6,7},{7,4},{8,9},{9,10},{10,1... | collective-permute-start | bytes 24584 | tf_op jit(solution)/shard_map/ppermute | solution.py:280
  41.8 0.1 pad_add_fusion.starts
  41.8 0.1 pad.3.clone
  41.9 9.6 %collective-permute-done.1 = bf16[128,32]{0,1:T(8,128)(2,1)S(1)} collective-permute-done((bf16[128,32]{0,1:T(8,128)(2,1)S(1)}, bf16[128,32]{0,1:T(8,128)(2,1)S(1)}, u32[]{:S(2)}, u32[]{:S(2)}) %collective-permute-start.1) | collective-permute-done | bytes 8224 | tf_op jit(solution)/shard_map/ppermute | solution.py:281
  51.5 0.0 collective-permute-done
  51.5 0.3 maximum_maximum_fusion.across
  51.8 23.4 %all-to-all-done.parts = bf16[512,4,384]{2,1,0:T(4,128)(2,1)S(1)} async-done(((bf16[512,4,384]{2,1,0:T(4,128)(2,1)}), bf16[512,4,384]{2,1,0:T(4,128)(2,1)S(1)}, u32[]{:S(2)}, u32[]{:S(2)}) %all-to-all-start) | async-done | bytes 1572896 | tf_op jit(solution)/shard_map/all_to_all | solution.py:275
  75.2 2.2 %correlate.1 = (bf16[128,1536]{1,0:T(8,128)(2,1)}, f32[8,128]{1,0:T(8,128)S(1)}) custom-call(s32[2]{0:T(128)S(1)} %pad_add_fusion.starts, bf16[512,4,384]{2,1,0:T(4,128)(2,1)S(1)} %all-to-all-done.parts, bf16[1664,128]{1,0:T(8,128)(2,1)S(1)} %maximum_maximum_fusion.across), custom_call_target="tpu_custom_call" | custom-call | tf_op jit(solution)/shard_map/correlate/pallas_call | solution.py:211
  77.3 10.1 %psum.7.totals = f32[8,128]{1,0:T(8,128)S(1)} all-reduce(f32[8,128]{1,0:T(8,128)S(1)} %get-tuple-element.10), channel_id=1, replica_groups=mesh['y'=8,'x'=4,'zh'=2,'co'=2,'zl'=4] {'zl'}, use_global_device_ids=true, to_apply=%region_0.0 | all-reduce | flops 1024 | bytes 8192 | tf_op jit(solution)/shard_map/psum | solution.py:287
  87.4 1.1 %finish.1 = (f32[1,4,16]{2,1,0:T(4,128)}, f32[1,2]{1,0:T(1,128)}) custom-call(s32[2]{0:T(128)S(1)} %pad_add_fusion.starts, f32[8,128]{1,0:T(8,128)S(1)} %psum.7.totals), custom_call_target="tpu_custom_call" | custom-call | tf_op jit(solution)/shard_map/finish/pallas_call | solution.py:245
  (2 shorter events, 0.0 us)
Async XLA Ops:
  10.4 21.2 %copy-start = (bf16[1,128,1536]{2,1,0:T(8,128)(2,1)S(1)}, bf16[1,128,1536]{2,1,0:T(8,128)(2,1)}, u32[]{:S(2)}) copy-start(bf16[1,128,1536]{2,1,0:T(8,128)(2,1)} %param.15) | copy-start | bytes 1179652
  10.4 64.7 %all-to-all-start = ((bf16[512,4,384]{2,1,0:T(4,128)(2,1)}), bf16[512,4,384]{2,1,0:T(4,128)(2,1)S(1)}, u32[]{:S(2)}, u32[]{:S(2)}) async-start(bf16[512,4,384]{2,1,0:T(4,128)(2,1)} %project.1), calls=%async_computation | async-start | bytes 3145728 | tf_op jit(solution)/shard_map/all_to_all | solution.py:275
  31.9 19.6 %collective-permute-start.1 = (bf16[128,32]{0,1:T(8,128)(2,1)S(1)}, bf16[128,32]{0,1:T(8,128)(2,1)S(1)}, u32[]{:S(2)}, u32[]{:S(2)}) collective-permute-start(bf16[128,32]{0,1:T(8,128)(2,1)S(1)} %get-tuple-element.14), channel_id=1, source_target_pairs={{1,0},{2,1},{3,2},{0,3},{5,4},{6,5},{7,6},{4,7},{9,8},{10,9},{11,1... | collective-permute-start | bytes 24584 | tf_op jit(solution)/shard_map/ppermute | solution.py:281
  38.5 12.9 %collective-permute-start = (bf16[128,32]{0,1:T(8,128)(2,1)S(1)}, bf16[128,32]{0,1:T(8,128)(2,1)S(1)}, u32[]{:S(2)}, u32[]{:S(2)}) collective-permute-start(bf16[128,32]{0,1:T(8,128)(2,1)S(1)} %get-tuple-element.13), channel_id=1, source_target_pairs={{0,1},{1,2},{2,3},{3,0},{4,5},{5,6},{6,7},{7,4},{8,9},{9,10},{10,1... | collective-permute-start | bytes 24584 | tf_op jit(solution)/shard_map/ppermute | solution.py:280

commit v5 on v4

--- a/solution.py
+++ b/solution.py
@@ -17,7 +17,7 @@
 
 def project_kernel(*refs):
     sources, out, rest = refs[:6], refs[6], refs[7:]
-    owner, shift, cls, weights, bank, volume, spreadable, held, mixed, ready, sems = rest
+    owner, shift, cls, weights, bank, volume, held, mixed, ready, sems = rest
     angles = weights.shape[0]
     columns = volume.shape[1]
     tile = bank.shape[1]
@@ -33,16 +33,8 @@
         pltpu.make_async_copy(source, target, sems.at[i])
         for i, (source, target) in enumerate(zip(sources[:5], rest[:5]))
     ]
-    large = []
-    for r in range(coarse // 2):
-        for j in range(ring):
-            where = pl.ds(j * coarse * tile + r * pair, pair)
-            large.append(
-                pltpu.make_async_copy(
-                    sources[5].at[:, where], volume.at[:, where], sems.at[5 + len(large)]
-                )
-            )
-    for copy in small + large:
+    large = pltpu.make_async_copy(sources[5], volume, sems.at[5])
+    for copy in small + [large]:
         copy.start()
     for copy in small:
         copy.wait()
@@ -56,39 +48,49 @@
         onehot.astype(jnp.bfloat16), weights[...], preferred_element_type=jnp.float32
     ).astype(jnp.bfloat16)
     classes = jnp.broadcast_to(classes, (angles, tile)).astype(jnp.int32)
-    masks = [(classes == c).astype(jnp.bfloat16) for c in range(banks)]
-    stacked = bank[...].reshape(banks * tile, tile)
+    beside = jnp.concatenate([bank[c] for c in range(banks)], axis=1)
     group = 8
+    block = 16
+    large.wait()
     for r in range(coarse // 2):
+        rays = []
         for j in range(ring):
-            large[r * ring + j].wait()
             at = j * coarse * tile + r * pair
-            ray = jnp.dot(
-                chosen, volume[:, at : at + pair], preferred_element_type=jnp.float32
-            ).astype(jnp.bfloat16)
-            for s in range(2):
-                piece = ray[:, s * tile : (s + 1) * tile]
-                for c in range(banks):
-                    spreadable[
-                        s, j * angles : (j + 1) * angles, c * tile : (c + 1) * tile
-                    ] = piece * masks[c]
+            rays.append(
+                jnp.dot(
+                    chosen, volume[:, at : at + pair], preferred_element_type=jnp.float32
+                ).astype(jnp.bfloat16)
+            )
         for s in range(2):
-            spread = jnp.dot(spreadable[s], stacked, preferred_element_type=jnp.float32)
-            for g in range(angles // group):
-                rows = slice(g * group, (g + 1) * group)
-                parts = [
-                    spread[j * angles + g * group : j * angles + (g + 1) * group]
-                    for j in range(ring)
-                ]
-                for b in range(3):
-                    keep = ((shifts[rows] >> (3 + b)) & 1) == 0
-                    parts = [
-                        jnp.where(keep, parts[j], parts[(j - (1 << b)) % ring])
-                        for j in range(ring)
-                    ]
-                for j in range(ring):
-                    at = (j * coarse + 2 * r + s) * tile
-                    held[rows, at : at + tile] = parts[j]
+            for first in range(0, angles, 128):
+                span = range(first, first + 128, block)
+                lhs = jnp.concatenate(
+                    [ray[k : k + block, s * tile : (s + 1) * tile] for k in span for ray in rays],
+                    axis=0,
+                )
+                spread = jnp.dot(lhs, beside, preferred_element_type=jnp.float32)
+                for i, k in enumerate(span):
+                    for half in range(block // group):
+                        rows = slice(k + half * group, k + (half + 1) * group)
+                        parts = []
+                        for j in range(ring):
+                            at = (i * ring + j) * block + half * group
+                            value = spread[at : at + group]
+                            part = value[:, :tile]
+                            for c in range(1, banks):
+                                part = jnp.where(
+                                    classes[rows] == c, value[:, c * tile : (c + 1) * tile], part
+                                )
+                            parts.append(part)
+                        for b in range(3):
+                            keep = ((shifts[rows] >> (3 + b)) & 1) == 0
+                            parts = [
+                                jnp.where(keep, parts[j], parts[(j - (1 << b)) % ring])
+                                for j in range(ring)
+                            ]
+                        for j in range(ring):
+                            at = (j * coarse + 2 * r + s) * tile
+                            held[rows, at : at + tile] = parts[j]
     inner = width // tile
     count = angles * strips
     copies = []
@@ -134,11 +136,10 @@
         out_specs=hbm,
         scratch_shapes=[pltpu.VMEM(x.shape, x.dtype) for x in small + (volume,)]
         + [
-            pltpu.VMEM((2, columns // tile // 8 * angles, bank.shape[0] * tile), jnp.bfloat16),
             pltpu.VMEM((angles, columns), jnp.float32),
             pltpu.VMEM((angles * columns // tile, tile), jnp.float32),
             pltpu.VMEM(shape, jnp.bfloat16),
-            pltpu.SemaphoreType.DMA((len(small) + columns // tile // 2,)),
+            pltpu.SemaphoreType.DMA((len(small) + 1,)),
         ],
         name="project",
     )(*small, volume)

time: 88.8 us -> 85.4 us (0.962)
  Pallas kernels: 13.1 us -> 9.66 us
    pallas_call x1, Pallas kernels: 9.76 us -> 6.34 us  [project(): pl.pallas_call(project_kernel, out_shape=jax.ShapeDtypeStruct(shape, jnp....]
where the time goes in v5:
time: 85.4 us; the launch traced here: 85.1 us
  waiting for transfers between devices  33 us (39%)
  starting transfers between devices  29.8 us (35%)
  blocking collectives  10.1 us (12%)
  Pallas kernels  9.66 us (11%)
  between operations  2 us (2%)
    all_to_all x1, waiting for transfers between devices, local(): lax.all_to_all(pieces, ('zl', 'y', 'x', 'zh', 'co'), 0, 0, tiled=True)  23.4 us
    all_to_all x1, starting transfers between devices, local(): lax.all_to_all(pieces, ('zl', 'y', 'x', 'zh', 'co'), 0, 0, tiled=True)  21.2 us
    psum x1, blocking collectives, local(): totals, shifts = finish(starts, lax.psum(part, 'zl'))  10.1 us
    ppermute x1, waiting for transfers between devices, local(): high = lax.ppermute(seen[:, :LAG], 'zl', back)  9.56 us
    ppermute x1, starting transfers between devices, local(): high = lax.ppermute(seen[:, :LAG], 'zl', back)  6.65 us
    pallas_call x1, Pallas kernels, project(): pl.pallas_call(project_kernel, out_shape=jax.ShapeDtypeStruct(shape, jnp....  6.34 us
    pallas_call x1, Pallas kernels, correlate(): pl.pallas_call(functools.partial(correlate_kernel, norm), out_shape=[jax....  2.17 us
    ppermute x1, starting transfers between devices, local(): low = lax.ppermute(seen[:, quarter - LAG:], 'zl', ring)  1.92 us
  transfers between devices with their start and end apart: 3, of which 2 were waited for; matrix products, arithmetic and copies ran while one was open for 1% of the time, Pallas kernels for 0%

profile of v5, /device:TPU:2, one launch (start us, length us, event | category | flops | bytes accessed | tf_op | source)
XLA Modules:
  0.0 85.1 jit_solution(847350381233203776)
XLA Ops:
  0.6 6.3 %project.1 = bf16[512,4,384]{2,1,0:T(4,128)(2,1)} custom-call(s32[1,128]{1,0:T(1,128)} %bitcast.15, s32[1,128]{1,0:T(1,128)} %bitcast.16, s32[1,128]{1,0:T(1,128)} %bitcast.17, bf16[128,128]{1,0:T(8,128)(2,1)} %refs_3_.1, bf16[4,128,128]{2,1,0:T(8,128)(2,1)} %refs_4_.1, bf16[128,6144]{1,0:T(8,128)(2,1)} %bitcast.12), custom_call_target="tpu_custom_call" | custom-call | tf_op jit(solution)/shard_map/project/pallas_call | solution.py:132
  7.0 0.0 copy-start
  7.0 21.2 %all-to-all-start = ((bf16[512,4,384]{2,1,0:T(4,128)(2,1)}), bf16[512,4,384]{2,1,0:T(4,128)(2,1)S(1)}, u32[]{:S(2)}, u32[]{:S(2)}) async-start(bf16[512,4,384]{2,1,0:T(4,128)(2,1)} %project.1), calls=%async_computation | async-start | bytes 3145728 | tf_op jit(solution)/shard_map/all_to_all | solution.py:276
  28.2 0.0 copy-done
  28.2 0.2 copy.12
  28.4 6.7 %collective-permute-start.1 = (bf16[128,32]{0,1:T(8,128)(2,1)S(1)}, bf16[128,32]{0,1:T(8,128)(2,1)S(1)}, u32[]{:S(2)}, u32[]{:S(2)}) collective-permute-start(bf16[128,32]{0,1:T(8,128)(2,1)S(1)} %get-tuple-element.14), channel_id=1, source_target_pairs={{1,0},{2,1},{3,2},{0,3},{5,4},{6,5},{7,6},{4,7},{9,8},{10,9},{11,1... | collective-permute-start | bytes 24584 | tf_op jit(solution)/shard_map/ppermute | solution.py:282
  35.1 1.9 %collective-permute-start = (bf16[128,32]{0,1:T(8,128)(2,1)S(1)}, bf16[128,32]{0,1:T(8,128)(2,1)S(1)}, u32[]{:S(2)}, u32[]{:S(2)}) collective-permute-start(bf16[128,32]{0,1:T(8,128)(2,1)S(1)} %get-tuple-element.13), channel_id=1, source_target_pairs={{0,1},{1,2},{2,3},{3,0},{4,5},{5,6},{6,7},{7,4},{8,9},{9,10},{10,1... | collective-permute-start | bytes 24584 | tf_op jit(solution)/shard_map/ppermute | solution.py:281
  38.3 0.1 pad_add_fusion.starts
  38.4 0.1 pad.3.clone
  38.5 9.6 %collective-permute-done.1 = bf16[128,32]{0,1:T(8,128)(2,1)S(1)} collective-permute-done((bf16[128,32]{0,1:T(8,128)(2,1)S(1)}, bf16[128,32]{0,1:T(8,128)(2,1)S(1)}, u32[]{:S(2)}, u32[]{:S(2)}) %collective-permute-start.1) | collective-permute-done | bytes 8224 | tf_op jit(solution)/shard_map/ppermute | solution.py:282
  48.1 0.0 collective-permute-done
  48.1 0.3 maximum_maximum_fusion.across
  48.3 23.4 %all-to-all-done.parts = bf16[512,4,384]{2,1,0:T(4,128)(2,1)S(1)} async-done(((bf16[512,4,384]{2,1,0:T(4,128)(2,1)}), bf16[512,4,384]{2,1,0:T(4,128)(2,1)S(1)}, u32[]{:S(2)}, u32[]{:S(2)}) %all-to-all-start) | async-done | bytes 1572896 | tf_op jit(solution)/shard_map/all_to_all | solution.py:276
  71.7 2.2 %correlate.1 = (bf16[128,1536]{1,0:T(8,128)(2,1)}, f32[8,128]{1,0:T(8,128)S(1)}) custom-call(s32[2]{0:T(128)S(1)} %pad_add_fusion.starts, bf16[512,4,384]{2,1,0:T(4,128)(2,1)S(1)} %all-to-all-done.parts, bf16[1664,128]{1,0:T(8,128)(2,1)S(1)} %maximum_maximum_fusion.across), custom_call_target="tpu_custom_call" | custom-call | tf_op jit(solution)/shard_map/correlate/pallas_call | solution.py:212
  73.9 10.1 %psum.7.totals = f32[8,128]{1,0:T(8,128)S(1)} all-reduce(f32[8,128]{1,0:T(8,128)S(1)} %get-tuple-element.10), channel_id=1, replica_groups=mesh['y'=8,'x'=4,'zh'=2,'co'=2,'zl'=4] {'zl'}, use_global_device_ids=true, to_apply=%region_0.0 | all-reduce | flops 1024 | bytes 8192 | tf_op jit(solution)/shard_map/psum | solution.py:288
  84.0 1.1 %finish.1 = (f32[1,4,16]{2,1,0:T(4,128)}, f32[1,2]{1,0:T(1,128)}) custom-call(s32[2]{0:T(128)S(1)} %pad_add_fusion.starts, f32[8,128]{1,0:T(8,128)S(1)} %psum.7.totals), custom_call_target="tpu_custom_call" | custom-call | tf_op jit(solution)/shard_map/finish/pallas_call | solution.py:246
  (2 shorter events, 0.0 us)
Async XLA Ops:
  7.0 21.2 %copy-start = (bf16[1,128,1536]{2,1,0:T(8,128)(2,1)S(1)}, bf16[1,128,1536]{2,1,0:T(8,128)(2,1)}, u32[]{:S(2)}) copy-start(bf16[1,128,1536]{2,1,0:T(8,128)(2,1)} %param.15) | copy-start | bytes 1179652
  7.0 64.7 %all-to-all-start = ((bf16[512,4,384]{2,1,0:T(4,128)(2,1)}), bf16[512,4,384]{2,1,0:T(4,128)(2,1)S(1)}, u32[]{:S(2)}, u32[]{:S(2)}) async-start(bf16[512,4,384]{2,1,0:T(4,128)(2,1)} %project.1), calls=%async_computation | async-start | bytes 3145728 | tf_op jit(solution)/shard_map/all_to_all | solution.py:276
  28.4 19.6 %collective-permute-start.1 = (bf16[128,32]{0,1:T(8,128)(2,1)S(1)}, bf16[128,32]{0,1:T(8,128)(2,1)S(1)}, u32[]{:S(2)}, u32[]{:S(2)}) collective-permute-start(bf16[128,32]{0,1:T(8,128)(2,1)S(1)} %get-tuple-element.14), channel_id=1, source_target_pairs={{1,0},{2,1},{3,2},{0,3},{5,4},{6,5},{7,6},{4,7},{9,8},{10,9},{11,1... | collective-permute-start | bytes 24584 | tf_op jit(solution)/shard_map/ppermute | solution.py:282
  35.1 12.9 %collective-permute-start = (bf16[128,32]{0,1:T(8,128)(2,1)S(1)}, bf16[128,32]{0,1:T(8,128)(2,1)S(1)}, u32[]{:S(2)}, u32[]{:S(2)}) collective-permute-start(bf16[128,32]{0,1:T(8,128)(2,1)S(1)} %get-tuple-element.13), channel_id=1, source_target_pairs={{0,1},{1,2},{2,3},{3,0},{4,5},{5,6},{6,7},{7,4},{8,9},{9,10},{10,1... | collective-permute-start | bytes 24584 | tf_op jit(solution)/shard_map/ppermute | solution.py:281

commit v6 on v5

--- a/solution.py
+++ b/solution.py
@@ -13,9 +13,10 @@
 LAGZ = 4
 WZ = 4
 ROWS = 144
-
-
-def project_kernel(*refs):
+EVERY = ("zl", "y", "x", "zh", "co")
+
+
+def project_kernel(quarters, *refs):
     sources, out, rest = refs[:6], refs[6], refs[7:]
     owner, shift, cls, weights, bank, volume, held, mixed, ready, sems = rest
     angles = weights.shape[0]
@@ -23,8 +24,6 @@
     tile = bank.shape[1]
     banks = bank.shape[0]
     tiles = columns // tile
-    peers, strips, width = ready.shape
-    quarters = peers // angles
     per = tiles // quarters
     coarse = 8
     ring = tiles // coarse
@@ -91,8 +90,7 @@
                         for j in range(ring):
                             at = (j * coarse + 2 * r + s) * tile
                             held[rows, at : at + tile] = parts[j]
-    inner = width // tile
-    count = angles * strips
+    count = angles * per
     copies = []
     for q in range(quarters):
         for g in range(angles // group):
@@ -108,14 +106,9 @@
                     jnp.where(keep, parts[i], parts[i - step]) for i in range(step, len(parts))
                 ]
             for c in range(per):
-                p, t = divmod(c, inner)
-                at = (q * inner + t) * count + g * group * strips + p
-                mixed[pl.ds(at, group, stride=strips), :] = parts[c]
-        where = slice(q * angles, (q + 1) * angles)
-        for t in range(inner):
-            at = (q * inner + t) * count
-            block = mixed[at : at + count].astype(jnp.bfloat16)
-            ready[where, :, t * tile : (t + 1) * tile] = block.reshape(angles, strips, tile)
+                mixed[pl.ds(q * count + g * group * per + c, group, stride=per), :] = parts[c]
+        where = slice(q * count, (q + 1) * count)
+        ready[where] = mixed[where].astype(jnp.bfloat16)
         copies.append(pltpu.make_async_copy(ready.at[where], out.at[where], sems.at[q]))
         copies[-1].start()
     for copy in copies:
@@ -126,18 +119,18 @@
     angles = weights.shape[0]
     columns = volume.shape[1]
     tile = bank.shape[1]
-    shape = (quarters * angles, 4, columns // quarters // 4)
+    shape = (angles * columns // tile, tile)
     small = (owner[None], shift[None], cls[None], weights, bank)
     hbm = pl.BlockSpec(memory_space=pltpu.HBM)
     return pl.pallas_call(
-        project_kernel,
+        functools.partial(project_kernel, quarters),
         out_shape=jax.ShapeDtypeStruct(shape, jnp.bfloat16),
         in_specs=[hbm] * 6,
         out_specs=hbm,
         scratch_shapes=[pltpu.VMEM(x.shape, x.dtype) for x in small + (volume,)]
         + [
             pltpu.VMEM((angles, columns), jnp.float32),
-            pltpu.VMEM((angles * columns // tile, tile), jnp.float32),
+            pltpu.VMEM(shape, jnp.float32),
             pltpu.VMEM(shape, jnp.bfloat16),
             pltpu.SemaphoreType.DMA((len(small) + 1,)),
         ],
@@ -146,29 +139,22 @@
 
 
 def correlate_kernel(norm, starts, parts, across, owned, out, mixed, wide):
-    peers, strips, width = parts.shape
     slices, columns = owned.shape
-    tile = 128
+    tile = parts.shape[1]
     tiles = columns // tile
-    inner = width // tile
-    count = slices * strips
-    group = 16
-    for g in range(slices // group):
-        total = jnp.zeros((group, strips, width), jnp.float32)
-        for c in range(peers // slices):
-            at = c * slices + g * group
-            total = total + parts[at : at + group].astype(jnp.float32)
-        for t in range(inner):
-            at = t * count + g * group * strips
-            block = total[:, :, t * tile : (t + 1) * tile]
-            mixed[at : at + group * strips] = block.reshape(group * strips, tile)
+    count = slices * tiles
+    group = 64
+    for at in range(0, count, group):
+        total = parts[at : at + group].astype(jnp.float32)
+        for c in range(1, parts.shape[0] // count):
+            block = parts[c * count + at : c * count + at + group]
+            total = total + block.astype(jnp.float32)
+        mixed[at : at + group] = total
     stack = []
-    for p in range(strips):
-        for t in range(inner):
-            block = mixed[pl.ds(t * count + p, slices, stride=strips), :].astype(jnp.bfloat16)
-            at = (p * inner + t) * tile
-            owned[:, at : at + tile] = block
-            stack.append(block)
+    for t in range(tiles):
+        block = mixed[pl.ds(t, slices, stride=tiles), :].astype(jnp.bfloat16)
+        owned[:, t * tile : (t + 1) * tile] = block
+        stack.append(block)
     rhs = jnp.concatenate(stack, axis=0)
     wide[...] = across[...].astype(jnp.float32)
     start_slice = starts[0]
@@ -205,9 +191,9 @@
     out[...] = jnp.concatenate(results, axis=0) * norm
 
 
-def correlate(norm, starts, parts, across):
-    peers, strips, width = parts.shape
-    slices, columns = across.shape[1], strips * width
+def correlate(norm, starts, parts, across, count):
+    slices = across.shape[1]
+    columns = parts.size // slices // count
     vmem = pl.BlockSpec(memory_space=pltpu.VMEM)
     return pl.pallas_call(
         functools.partial(correlate_kernel, norm),
@@ -273,7 +259,10 @@
     pieces = project(
         owner_angle, tile_shift, tile_class, detector_row_weight, tile_bank, volume[0], count
     )
-    parts = lax.all_to_all(pieces, ("zl", "y", "x", "zh", "co"), 0, 0, tiled=True)
+    peers = math.prod(lax.axis_size(axis) for axis in EVERY)
+    parts = lax.all_to_all(
+        pieces.reshape(-1, 4, 128).reshape(peers, -1, 4, 128), EVERY, 0, 0, tiled=True
+    ).reshape(-1, 4, 128).reshape(pieces.shape)
     seen, _ = lax.optimization_barrier((measured[0], pieces))
     slices, quarter = seen.shape
     ring = [(i, (i + 1) % count) for i in range(count)]
@@ -284,7 +273,7 @@
     across = jnp.concatenate([low.T, seen.T, high.T, rest], axis=0)
     starts = jnp.concatenate([window_slice, window_col])
     norm_factor = 1.0 / math.sqrt(slices * quarter * count)
-    owned, part = correlate(norm_factor, starts, parts, across)
+    owned, part = correlate(norm_factor, starts, parts, across, count)
     totals, shifts = finish(starts, lax.psum(part, "zl"))
     return (owned[None], totals, shifts.T)
 

time: 85.4 us -> 84.9 us (level)
  no operation moved by 1% of the time
where the time goes in v6:
time: 84.9 us; the launch traced here: 84.6 us
  waiting for transfers between devices  33 us (39%)
  starting transfers between devices  29.8 us (35%)
  blocking collectives  10.1 us (12%)
  Pallas kernels  9.12 us (11%)
  between operations  2 us (2%)
    all_to_all x1, waiting for transfers between devices, local(): lax.all_to_all(pieces.reshape(-1, 4, 128).reshape(peers, -1, 4, 128), EVE...  23.4 us
    all_to_all x1, starting transfers between devices, local(): lax.all_to_all(pieces.reshape(-1, 4, 128).reshape(peers, -1, 4, 128), EVE...  21.2 us
    psum x1, blocking collectives, local(): totals, shifts = finish(starts, lax.psum(part, 'zl'))  10.1 us
    ppermute x1, waiting for transfers between devices, local(): high = lax.ppermute(seen[:, :LAG], 'zl', back)  9.56 us
    ppermute x1, starting transfers between devices, local(): high = lax.ppermute(seen[:, :LAG], 'zl', back)  6.65 us
    pallas_call x1, Pallas kernels, project(): pl.pallas_call(functools.partial(project_kernel, quarters), out_shape=jax...  6.01 us
    pallas_call x1, Pallas kernels, correlate(): pl.pallas_call(functools.partial(correlate_kernel, norm), out_shape=[jax....  1.96 us
    ppermute x1, starting transfers between devices, local(): low = lax.ppermute(seen[:, quarter - LAG:], 'zl', ring)  1.92 us
  transfers between devices with their start and end apart: 3, of which 2 were waited for; matrix products, arithmetic and copies ran while one was open for 1% of the time, Pallas kernels for 0%

profile of v6, /device:TPU:2, one launch (start us, length us, event | category | flops | bytes accessed | tf_op | source)
XLA Modules:
  0.0 84.6 jit_solution(14927511980522981135)
XLA Ops:
  0.6 6.0 %project.1 = bf16[6144,128]{1,0:T(8,128)(2,1)} custom-call(s32[1,128]{1,0:T(1,128)} %bitcast.19, s32[1,128]{1,0:T(1,128)} %bitcast.20, s32[1,128]{1,0:T(1,128)} %bitcast.21, bf16[128,128]{1,0:T(8,128)(2,1)} %refs_3_.1, bf16[4,128,128]{2,1,0:T(8,128)(2,1)} %refs_4_.1, bf16[128,6144]{1,0:T(8,128)(2,1)} %bitcast.16), custom_call_target="tpu_custom_call" | custom-call | tf_op jit(solution)/shard_map/project/pallas_call | solution.py:125
  6.7 0.0 copy-start
  6.7 21.2 %all-to-all-start = ((bf16[512,3,4,128]{3,2,1,0:T(4,128)(2,1)}), bf16[512,3,4,128]{3,2,1,0:T(4,128)(2,1)S(1)}, u32[]{:S(2)}, u32[]{:S(2)}) async-start(bf16[512,3,4,128]{3,2,1,0:T(4,128)(2,1)} %bitcast.13), calls=%async_computation | async-start | bytes 3145728 | tf_op jit(solution)/shard_map/all_to_all | solution.py:263
  27.9 0.0 copy-done
  27.9 0.2 copy.12
  28.1 6.7 %collective-permute-start.1 = (bf16[128,32]{0,1:T(8,128)(2,1)S(1)}, bf16[128,32]{0,1:T(8,128)(2,1)S(1)}, u32[]{:S(2)}, u32[]{:S(2)}) collective-permute-start(bf16[128,32]{0,1:T(8,128)(2,1)S(1)} %get-tuple-element.14), channel_id=1, source_target_pairs={{1,0},{2,1},{3,2},{0,3},{5,4},{6,5},{7,6},{4,7},{9,8},{10,9},{11,1... | collective-permute-start | bytes 24584 | tf_op jit(solution)/shard_map/ppermute | solution.py:271
  34.8 1.9 %collective-permute-start = (bf16[128,32]{0,1:T(8,128)(2,1)S(1)}, bf16[128,32]{0,1:T(8,128)(2,1)S(1)}, u32[]{:S(2)}, u32[]{:S(2)}) collective-permute-start(bf16[128,32]{0,1:T(8,128)(2,1)S(1)} %get-tuple-element.13), channel_id=1, source_target_pairs={{0,1},{1,2},{2,3},{3,0},{4,5},{5,6},{6,7},{7,4},{8,9},{9,10},{10,1... | collective-permute-start | bytes 24584 | tf_op jit(solution)/shard_map/ppermute | solution.py:270
  38.0 0.1 pad_add_fusion.starts
  38.1 0.1 pad.3.clone
  38.2 9.6 %collective-permute-done.1 = bf16[128,32]{0,1:T(8,128)(2,1)S(1)} collective-permute-done((bf16[128,32]{0,1:T(8,128)(2,1)S(1)}, bf16[128,32]{0,1:T(8,128)(2,1)S(1)}, u32[]{:S(2)}, u32[]{:S(2)}) %collective-permute-start.1) | collective-permute-done | bytes 8224 | tf_op jit(solution)/shard_map/ppermute | solution.py:271
  47.7 0.0 collective-permute-done
  47.7 0.3 maximum_maximum_fusion.across
  48.0 23.4 %all-to-all-done = bf16[512,3,4,128]{3,2,1,0:T(4,128)(2,1)S(1)} async-done(((bf16[512,3,4,128]{3,2,1,0:T(4,128)(2,1)}), bf16[512,3,4,128]{3,2,1,0:T(4,128)(2,1)S(1)}, u32[]{:S(2)}, u32[]{:S(2)}) %all-to-all-start) | async-done | bytes 1572896 | tf_op jit(solution)/shard_map/all_to_all | solution.py:263
  71.4 2.0 %correlate.1 = (bf16[128,1536]{1,0:T(8,128)(2,1)}, f32[8,128]{1,0:T(8,128)S(1)}) custom-call(s32[2]{0:T(128)S(1)} %pad_add_fusion.starts, bf16[6144,128]{1,0:T(8,128)(2,1)S(1)} %bitcast.12, bf16[1664,128]{1,0:T(8,128)(2,1)S(1)} %maximum_maximum_fusion.across), custom_call_target="tpu_custom_call" | custom-call | tf_op jit(solution)/shard_map/correlate/pallas_call | solution.py:198
  73.4 10.1 %psum.7.totals = f32[8,128]{1,0:T(8,128)S(1)} all-reduce(f32[8,128]{1,0:T(8,128)S(1)} %get-tuple-element.10), channel_id=1, replica_groups=mesh['y'=8,'x'=4,'zh'=2,'co'=2,'zl'=4] {'zl'}, use_global_device_ids=true, to_apply=%region_0.0 | all-reduce | flops 1024 | bytes 8192 | tf_op jit(solution)/shard_map/psum | solution.py:277
  83.4 1.1 %finish.1 = (f32[1,4,16]{2,1,0:T(4,128)}, f32[1,2]{1,0:T(1,128)}) custom-call(s32[2]{0:T(128)S(1)} %pad_add_fusion.starts, f32[8,128]{1,0:T(8,128)S(1)} %psum.7.totals), custom_call_target="tpu_custom_call" | custom-call | tf_op jit(solution)/shard_map/finish/pallas_call | solution.py:232
  (2 shorter events, 0.0 us)
Async XLA Ops:
  6.7 21.2 %copy-start = (bf16[1,128,1536]{2,1,0:T(8,128)(2,1)S(1)}, bf16[1,128,1536]{2,1,0:T(8,128)(2,1)}, u32[]{:S(2)}) copy-start(bf16[1,128,1536]{2,1,0:T(8,128)(2,1)} %param.15) | copy-start | bytes 1179652
  6.7 64.7 %all-to-all-start = ((bf16[512,3,4,128]{3,2,1,0:T(4,128)(2,1)}), bf16[512,3,4,128]{3,2,1,0:T(4,128)(2,1)S(1)}, u32[]{:S(2)}, u32[]{:S(2)}) async-start(bf16[512,3,4,128]{3,2,1,0:T(4,128)(2,1)} %bitcast.13), calls=%async_computation | async-start | bytes 3145728 | tf_op jit(solution)/shard_map/all_to_all | solution.py:263
  28.1 19.6 %collective-permute-start.1 = (bf16[128,32]{0,1:T(8,128)(2,1)S(1)}, bf16[128,32]{0,1:T(8,128)(2,1)S(1)}, u32[]{:S(2)}, u32[]{:S(2)}) collective-permute-start(bf16[128,32]{0,1:T(8,128)(2,1)S(1)} %get-tuple-element.14), channel_id=1, source_target_pairs={{1,0},{2,1},{3,2},{0,3},{5,4},{6,5},{7,6},{4,7},{9,8},{10,9},{11,1... | collective-permute-start | bytes 24584 | tf_op jit(solution)/shard_map/ppermute | solution.py:271
  34.8 12.9 %collective-permute-start = (bf16[128,32]{0,1:T(8,128)(2,1)S(1)}, bf16[128,32]{0,1:T(8,128)(2,1)S(1)}, u32[]{:S(2)}, u32[]{:S(2)}) collective-permute-start(bf16[128,32]{0,1:T(8,128)(2,1)S(1)} %get-tuple-element.13), channel_id=1, source_target_pairs={{0,1},{1,2},{2,3},{3,0},{4,5},{5,6},{6,7},{7,4},{8,9},{9,10},{10,1... | collective-permute-start | bytes 24584 | tf_op jit(solution)/shard_map/ppermute | solution.py:270

commit v7 on v6

--- a/solution.py
+++ b/solution.py
@@ -138,7 +138,33 @@
     )(*small, volume)
 
 
-def correlate_kernel(norm, starts, parts, across, owned, out, mixed, wide):
+def align_kernel(starts, across, lhs, wide):
+    slices = across.shape[1]
+    tiles = lhs.shape[1] // slices
+    wide[...] = across[...].astype(jnp.float32)
+    first = starts[1] + LAG
+    for a in range(WZ):
+        turn = lax.rem(2 * slices - starts[0] - a, slices)
+        for t in range(tiles):
+            block = wide[pl.ds(first + t * slices, ROWS), :]
+            lhs[a * ROWS : (a + 1) * ROWS, t * slices : (t + 1) * slices] = pltpu.roll(
+                block, turn, 1
+            ).astype(jnp.bfloat16)
+
+
+def align(starts, across, tiles):
+    vmem = pl.BlockSpec(memory_space=pltpu.VMEM)
+    return pl.pallas_call(
+        align_kernel,
+        out_shape=jax.ShapeDtypeStruct((WZ * ROWS, tiles * across.shape[1]), jnp.bfloat16),
+        in_specs=[pl.BlockSpec(memory_space=pltpu.SMEM), vmem],
+        scratch_shapes=[pltpu.VMEM(across.shape, jnp.float32)],
+        compiler_params=pltpu.CompilerParams(vmem_limit_bytes=8 * 2**20),
+        name="align",
+    )(starts, across)
+
+
+def correlate_kernel(norm, parts, lhs, owned, out, mixed, ready, sem):
     slices, columns = owned.shape
     tile = parts.shape[1]
     tiles = columns // tile
@@ -153,22 +179,12 @@
     stack = []
     for t in range(tiles):
         block = mixed[pl.ds(t, slices, stride=tiles), :].astype(jnp.bfloat16)
-        owned[:, t * tile : (t + 1) * tile] = block
+        ready[:, t * tile : (t + 1) * tile] = block
         stack.append(block)
+    copy = pltpu.make_async_copy(ready, owned, sem.at[0])
+    copy.start()
     rhs = jnp.concatenate(stack, axis=0)
-    wide[...] = across[...].astype(jnp.float32)
-    start_slice = starts[0]
-    first = starts[1] + LAG
-    pieces = []
-    for a in range(WZ):
-        turn = lax.rem(2 * slices - start_slice - a, slices)
-        row = []
-        for t in range(tiles):
-            block = wide[pl.ds(first + t * tile, ROWS), :]
-            row.append(pltpu.roll(block, turn, 1).astype(jnp.bfloat16))
-        pieces.append(jnp.concatenate(row, axis=1))
-    lhs = jnp.concatenate(pieces, axis=0)
-    sums = jnp.dot(lhs, rhs, preferred_element_type=jnp.float32)
+    sums = jnp.dot(lhs[...], rhs, preferred_element_type=jnp.float32)
     lanes = lax.broadcasted_iota(jnp.int32, (8, tile), 1)
     subs = lax.broadcasted_iota(jnp.int32, (8, tile), 0)
     results = []
@@ -188,31 +204,37 @@
             aligned = jnp.where(lanes == d, value, aligned)
         results.append(aligned[0:1])
     results.append(jnp.zeros((8 - WZ, tile), jnp.float32))
-    out[...] = jnp.concatenate(results, axis=0) * norm
-
-
-def correlate(norm, starts, parts, across, count):
-    slices = across.shape[1]
-    columns = parts.size // slices // count
+    values = jnp.concatenate(results, axis=0) * norm
+    for peer in range(out.shape[0]):
+        out[peer] = values
+    copy.wait()
+
+
+def correlate(norm, parts, lhs, count):
+    slices = parts.size // count // lhs.shape[1]
     vmem = pl.BlockSpec(memory_space=pltpu.VMEM)
     return pl.pallas_call(
         functools.partial(correlate_kernel, norm),
         out_shape=[
-            jax.ShapeDtypeStruct((slices, columns), jnp.bfloat16),
-            jax.ShapeDtypeStruct((8, 128), jnp.float32),
-        ],
-        in_specs=[pl.BlockSpec(memory_space=pltpu.SMEM), vmem, vmem],
+            jax.ShapeDtypeStruct((slices, lhs.shape[1]), jnp.bfloat16),
+            jax.ShapeDtypeStruct((count, 8, 128), jnp.float32),
+        ],
+        in_specs=[vmem, vmem],
+        out_specs=[pl.BlockSpec(memory_space=pltpu.HBM), vmem],
         scratch_shapes=[
-            pltpu.VMEM((slices * columns // 128, 128), jnp.float32),
-            pltpu.VMEM(across.shape, jnp.float32),
+            pltpu.VMEM((parts.shape[0] // count, parts.shape[1]), jnp.float32),
+            pltpu.VMEM((slices, lhs.shape[1]), jnp.bfloat16),
+            pltpu.SemaphoreType.DMA((1,)),
         ],
         compiler_params=pltpu.CompilerParams(vmem_limit_bytes=14 * 2**20),
         name="correlate",
-    )(starts, parts, across)
+    )(parts, lhs)
 
 
 def finish_kernel(starts, totals, correlation, shifts):
-    values = totals[0:WZ, 0:WU]
+    values = totals[0, 0:WZ, 0:WU]
+    for c in range(1, totals.shape[0]):
+        values = values + totals[c, 0:WZ, 0:WU]
     correlation[0] = values
     weights = values * values
     lag_slice = starts[0] + lax.broadcasted_iota(jnp.int32, (WZ, WU), 0)
@@ -273,8 +295,10 @@
     across = jnp.concatenate([low.T, seen.T, high.T, rest], axis=0)
     starts = jnp.concatenate([window_slice, window_col])
     norm_factor = 1.0 / math.sqrt(slices * quarter * count)
-    owned, part = correlate(norm_factor, starts, parts, across, count)
-    totals, shifts = finish(starts, lax.psum(part, "zl"))
+    lhs = align(starts, across, quarter // slices)
+    owned, part = correlate(norm_factor, parts, lhs, count)
+    shares = lax.all_to_all(part, "zl", 0, 0, tiled=True)
+    totals, shifts = finish(starts, shares)
     return (owned[None], totals, shifts.T)
 
 

time: 84.9 us -> 82.9 us (0.976)
  blocking collectives: 10.1 us -> 8.41 us
  waiting for transfers between devices: 33 us -> 31.8 us
    psum x1 -> x0, blocking collectives: 10.1 us -> none  [local(): totals, shifts = finish(starts, lax.psum(part, 'zl'))]
    ppermute x1, waiting for transfers between devices: 0.01 us -> 8.62 us  [local(): low = lax.ppermute(seen[:, quarter - LAG:], 'zl', ring)]
    ppermute x1, waiting for transfers between devices: 9.56 us -> 0.95 us  [local(): high = lax.ppermute(seen[:, :LAG], 'zl', back)]
    all_to_all x0 -> x1, blocking collectives: none -> 8.41 us  [local(): shares = lax.all_to_all(part, 'zl', 0, 0, tiled=True)]
    ppermute x1, starting transfers between devices: 1.92 us -> 3.78 us  [local(): low = lax.ppermute(seen[:, quarter - LAG:], 'zl', ring)]
    ppermute x1, starting transfers between devices: 6.65 us -> 4.8 us  [local(): high = lax.ppermute(seen[:, :LAG], 'zl', back)]
    all_to_all x1, waiting for transfers between devices: 23.4 us -> 22.3 us  [local(): lax.all_to_all(pieces.reshape(-1, 4, 128).reshape(peers, -1, 4, 128), EVE...]
    pallas_call x0 -> x1, Pallas kernels: none -> 1.12 us  [align(): pl.pallas_call(align_kernel, out_shape=jax.ShapeDtypeStruct((WZ * ROWS, t...]
  transfers between devices with their start and end apart: 3 -> 3, of which waited for: 2 -> 3; matrix products, arithmetic and copies ran while one was open for 1% -> 1% of each run, Pallas kernels for 0% -> 1%
where the time goes in v7:
time: 82.9 us; the launch traced here: 82.6 us
  waiting for transfers between devices  31.8 us (38%)
  starting transfers between devices  29.8 us (36%)
  Pallas kernels  9.92 us (12%)
  blocking collectives  8.41 us (10%)
  between operations  2.01 us (2%)
    all_to_all x1, waiting for transfers between devices, local(): lax.all_to_all(pieces.reshape(-1, 4, 128).reshape(peers, -1, 4, 128), EVE...  22.3 us
    all_to_all x1, starting transfers between devices, local(): lax.all_to_all(pieces.reshape(-1, 4, 128).reshape(peers, -1, 4, 128), EVE...  21.2 us
    ppermute x1, waiting for transfers between devices, local(): low = lax.ppermute(seen[:, quarter - LAG:], 'zl', ring)  8.62 us
    all_to_all x1, blocking collectives, local(): shares = lax.all_to_all(part, 'zl', 0, 0, tiled=True)  8.41 us
    pallas_call x1, Pallas kernels, project(): pl.pallas_call(functools.partial(project_kernel, quarters), out_shape=jax...  6 us
    ppermute x1, starting transfers between devices, local(): high = lax.ppermute(seen[:, :LAG], 'zl', back)  4.8 us
    ppermute x1, starting transfers between devices, local(): low = lax.ppermute(seen[:, quarter - LAG:], 'zl', ring)  3.78 us
  transfers between devices with their start and end apart: 3, of which 3 were waited for; matrix products, arithmetic and copies ran while one was open for 1% of the time, Pallas kernels for 1%

profile of v7, /device:TPU:2, one launch (start us, length us, event | category | flops | bytes accessed | tf_op | source)
XLA Modules:
  0.0 82.6 jit_solution(5211062894941535758)
XLA Ops:
  0.6 6.0 %project.1 = bf16[6144,128]{1,0:T(8,128)(2,1)} custom-call(s32[1,128]{1,0:T(1,128)} %bitcast.19, s32[1,128]{1,0:T(1,128)} %bitcast.20, s32[1,128]{1,0:T(1,128)} %bitcast.21, bf16[128,128]{1,0:T(8,128)(2,1)} %refs_3_.1, bf16[4,128,128]{2,1,0:T(8,128)(2,1)} %refs_4_.1, bf16[128,6144]{1,0:T(8,128)(2,1)} %bitcast.16), custom_call_target="tpu_custom_call" | custom-call | tf_op jit(solution)/shard_map/project/pallas_call | solution.py:125
  6.6 0.0 copy-start
  6.7 21.2 %all-to-all-start = ((bf16[512,3,4,128]{3,2,1,0:T(4,128)(2,1)}), bf16[512,3,4,128]{3,2,1,0:T(4,128)(2,1)S(1)}, u32[]{:S(2)}, u32[]{:S(2)}) async-start(bf16[512,3,4,128]{3,2,1,0:T(4,128)(2,1)} %bitcast.13), calls=%async_computation | async-start | bytes 3145728 | tf_op jit(solution)/shard_map/all_to_all | solution.py:285
  27.9 0.0 copy-done
  27.9 0.2 copy.12
  28.1 3.8 %collective-permute-start = (bf16[128,32]{0,1:T(8,128)(2,1)S(1)}, bf16[128,32]{0,1:T(8,128)(2,1)S(1)}, u32[]{:S(2)}, u32[]{:S(2)}) collective-permute-start(bf16[128,32]{0,1:T(8,128)(2,1)S(1)} %get-tuple-element.13), channel_id=1, source_target_pairs={{0,1},{1,2},{2,3},{3,0},{4,5},{5,6},{6,7},{7,4},{8,9},{9,10},{10,1... | collective-permute-start | bytes 24584 | tf_op jit(solution)/shard_map/ppermute | solution.py:292
  31.9 4.8 %collective-permute-start.1 = (bf16[128,32]{0,1:T(8,128)(2,1)S(1)}, bf16[128,32]{0,1:T(8,128)(2,1)S(1)}, u32[]{:S(2)}, u32[]{:S(2)}) collective-permute-start(bf16[128,32]{0,1:T(8,128)(2,1)S(1)} %get-tuple-element.14), channel_id=1, source_target_pairs={{1,0},{2,1},{3,2},{0,3},{5,4},{6,5},{7,6},{4,7},{9,8},{10,9},{11,1... | collective-permute-start | bytes 24584 | tf_op jit(solution)/shard_map/ppermute | solution.py:293
  38.0 0.1 pad_add_fusion.starts
  38.1 0.1 pad.3.clone
  38.1 8.6 %collective-permute-done = bf16[128,32]{0,1:T(8,128)(2,1)S(1)} collective-permute-done((bf16[128,32]{0,1:T(8,128)(2,1)S(1)}, bf16[128,32]{0,1:T(8,128)(2,1)S(1)}, u32[]{:S(2)}, u32[]{:S(2)}) %collective-permute-start) | collective-permute-done | bytes 8224 | tf_op jit(solution)/shard_map/ppermute | solution.py:292
  46.8 1.0 %collective-permute-done.1 = bf16[128,32]{0,1:T(8,128)(2,1)S(1)} collective-permute-done((bf16[128,32]{0,1:T(8,128)(2,1)S(1)}, bf16[128,32]{0,1:T(8,128)(2,1)S(1)}, u32[]{:S(2)}, u32[]{:S(2)}) %collective-permute-start.1) | collective-permute-done | bytes 8224 | tf_op jit(solution)/shard_map/ppermute | solution.py:293
  47.7 0.3 maximum_maximum_fusion.across
  48.0 1.1 %align.1.lhs = bf16[576,1536]{1,0:T(8,128)(2,1)S(1)} custom-call(s32[2]{0:T(128)S(1)} %pad_add_fusion.starts, bf16[1664,128]{1,0:T(8,128)(2,1)S(1)} %maximum_maximum_fusion.across), custom_call_target="tpu_custom_call" | custom-call | tf_op jit(solution)/shard_map/align/pallas_call | solution.py:157
  49.1 22.3 %all-to-all-done = bf16[512,3,4,128]{3,2,1,0:T(4,128)(2,1)S(1)} async-done(((bf16[512,3,4,128]{3,2,1,0:T(4,128)(2,1)}), bf16[512,3,4,128]{3,2,1,0:T(4,128)(2,1)S(1)}, u32[]{:S(2)}, u32[]{:S(2)}) %all-to-all-start) | async-done | bytes 1572896 | tf_op jit(solution)/shard_map/all_to_all | solution.py:285
  71.4 1.7 %correlate.1 = (bf16[128,1536]{1,0:T(8,128)(2,1)}, f32[4,8,128]{2,1,0:T(8,128)S(1)}) custom-call(bf16[6144,128]{1,0:T(8,128)(2,1)S(1)} %bitcast.12, bf16[576,1536]{1,0:T(8,128)(2,1)S(1)} %align.1.lhs), custom_call_target="tpu_custom_call" | custom-call | tf_op jit(solution)/shard_map/correlate/pallas_call | solution.py:216
  73.1 8.4 %all_to_all.10.totals = f32[4,8,128]{2,1,0:T(8,128)S(1)} all-to-all(f32[4,8,128]{2,1,0:T(8,128)S(1)} %get-tuple-element.10), channel_id=1, replica_groups=mesh['y'=8,'x'=4,'zh'=2,'co'=2,'zl'=4] {'zl'}, dimensions={0} | all-to-all | bytes 32768 | tf_op jit(solution)/shard_map/all_to_all | solution.py:300
  81.5 1.1 %finish.1 = (f32[1,4,16]{2,1,0:T(4,128)}, f32[1,2]{1,0:T(1,128)}) custom-call(s32[2]{0:T(128)S(1)} %pad_add_fusion.starts, f32[4,8,128]{2,1,0:T(8,128)S(1)} %all_to_all.10.totals), custom_call_target="tpu_custom_call" | custom-call | tf_op jit(solution)/shard_map/finish/pallas_call | solution.py:254
  (2 shorter events, 0.0 us)
Async XLA Ops:
  6.6 21.2 %copy-start = (bf16[1,128,1536]{2,1,0:T(8,128)(2,1)S(1)}, bf16[1,128,1536]{2,1,0:T(8,128)(2,1)}, u32[]{:S(2)}) copy-start(bf16[1,128,1536]{2,1,0:T(8,128)(2,1)} %param.15) | copy-start | bytes 1179652
  6.7 64.7 %all-to-all-start = ((bf16[512,3,4,128]{3,2,1,0:T(4,128)(2,1)}), bf16[512,3,4,128]{3,2,1,0:T(4,128)(2,1)S(1)}, u32[]{:S(2)}, u32[]{:S(2)}) async-start(bf16[512,3,4,128]{3,2,1,0:T(4,128)(2,1)} %bitcast.13), calls=%async_computation | async-start | bytes 3145728 | tf_op jit(solution)/shard_map/all_to_all | solution.py:285
  28.1 18.7 %collective-permute-start = (bf16[128,32]{0,1:T(8,128)(2,1)S(1)}, bf16[128,32]{0,1:T(8,128)(2,1)S(1)}, u32[]{:S(2)}, u32[]{:S(2)}) collective-permute-start(bf16[128,32]{0,1:T(8,128)(2,1)S(1)} %get-tuple-element.13), channel_id=1, source_target_pairs={{0,1},{1,2},{2,3},{3,0},{4,5},{5,6},{6,7},{7,4},{8,9},{9,10},{10,1... | collective-permute-start | bytes 24584 | tf_op jit(solution)/shard_map/ppermute | solution.py:292
  31.9 15.8 %collective-permute-start.1 = (bf16[128,32]{0,1:T(8,128)(2,1)S(1)}, bf16[128,32]{0,1:T(8,128)(2,1)S(1)}, u32[]{:S(2)}, u32[]{:S(2)}) collective-permute-start(bf16[128,32]{0,1:T(8,128)(2,1)S(1)} %get-tuple-element.14), channel_id=1, source_target_pairs={{1,0},{2,1},{3,2},{0,3},{5,4},{6,5},{7,6},{4,7},{9,8},{10,9},{11,1... | collective-permute-start | bytes 24584 | tf_op jit(solution)/shard_map/ppermute | solution.py:293
